TPU v7x, 32 devices: a 4x4x1 block of a 4x4x8 slice. The times are simulated.
32 devices in a mesh: dp: 1 (over z), tp: 4 (over y), cp: 8 (over x, core).
Axes of the slice: x: 4, y: 4, z: 1, core: 2. Of those that a mesh axis runs over, the one named last changes fastest.
The devices are a block of a 4x4x8 slice.
Arguments:
- x_suffix: bfloat16 [8192, 3072], P(('dp', 'cp'))
- k_prefix: bfloat16 [8192, 8, 128], P(('dp', 'cp'), 'tp')
- v_prefix: bfloat16 [8192, 8, 128], P(('dp', 'cp'), 'tp')
- norm_attn: bfloat16 [3072], replicated
- w_query: bfloat16 [3072, 3072], P(None, 'tp')
- w_key: bfloat16 [3072, 1024], P(None, 'tp')
- w_value: bfloat16 [3072, 1024], P(None, 'tp')
- w_out: bfloat16 [3072, 3072], P('tp')
- norm_mlp: bfloat16 [3072], replicated
- w_gate: bfloat16 [3072, 8192], P(None, 'tp')
- w_up: bfloat16 [3072, 8192], P(None, 'tp')
- w_down: bfloat16 [8192, 3072], P('tp')
Outputs:
- output 1: bfloat16 [8192, 3072], P(('dp', 'cp'))
- output 2: bfloat16 [8192, 8, 128], P(('dp', 'cp'), 'tp')
- output 3: bfloat16 [8192, 8, 128], P(('dp', 'cp'), 'tp')
All inputs are finite; a program needn't handle non-finite values.
Results may differ from a plain program's by a relative error of at most 0.0109944.
Values are sent between devices in bfloat16 or wider.
A program may use at most 768 MiB of HBM per device.

v0:
```python
import jax
import jax.numpy as jnp
from jax import lax
from jax.sharding import PartitionSpec as P

ROPE_THETA = 500000.0
NORM_EPS = 1e-5


def block_positions(owner, groups, blk_len, prefix_len):
    local_row = jnp.arange(2 * blk_len, dtype=jnp.int32)
    blk_idx = jnp.where(local_row < blk_len, owner, 2 * groups - 1 - owner)
    return prefix_len + blk_idx * blk_len + local_row % blk_len


def rope_tables(positions, head_dim):
    inv_freq = ROPE_THETA ** (-jnp.arange(0, head_dim, 2, dtype=jnp.float32) / head_dim)
    angles = positions.astype(jnp.float32)[:, None] * inv_freq[None, :]
    return jnp.cos(angles), jnp.sin(angles)


def apply_rope(values, cos_tab, sin_tab):
    half_dim = values.shape[-1] // 2
    first_half = values[..., :half_dim]
    second_half = values[..., half_dim:]
    cos_rows = cos_tab[:, None, :]
    sin_rows = sin_tab[:, None, :]
    return jnp.concatenate([first_half * cos_rows - second_half * sin_rows, second_half * cos_rows + first_half * sin_rows], axis=-1)


def rms_norm(values, gain_vec):
    vals32 = values.astype(jnp.float32)
    inv_rms = lax.rsqrt(jnp.mean(vals32 * vals32, axis=-1, keepdims=True) + NORM_EPS)
    return (vals32 * inv_rms * gain_vec.astype(jnp.float32)).astype(jnp.bfloat16)


def attend_step(acc_state, q_rot, k_blk, v_blk, q_pos, k_pos, score_scale):
    row_max, denom_sum, numer_sum = acc_state
    scores = jnp.einsum('sgrd,kgd->sgrk', q_rot, k_blk, preferred_element_type=jnp.float32) * score_scale
    visible = (k_pos[None, :] <= q_pos[:, None])[:, None, None, :]
    scores = jnp.where(visible, scores, -jnp.inf)
    new_max = jnp.maximum(row_max, jnp.max(scores, axis=-1))
    correction = jnp.exp(row_max - new_max)
    weights = jnp.exp(scores - new_max[..., None])
    denom_sum = denom_sum * correction + jnp.sum(weights, axis=-1)
    numer_sum = numer_sum * correction[..., None] + jnp.einsum('sgrk,kgd->sgrd', weights.astype(jnp.bfloat16), v_blk, preferred_element_type=jnp.float32)
    return new_max, denom_sum, numer_sum


def solution(mesh):
    groups = mesh.shape['cp']

    def local_layer(x_loc, kp_loc, vp_loc, norm_attn, w_query, w_key, w_value, w_out, norm_mlp, w_gate, w_up, w_down):
        rows_loc = x_loc.shape[0]
        blk_len = rows_loc // 2
        pre_dev, kv_loc, head_dim = kp_loc.shape
        heads_loc = w_query.shape[1] // head_dim
        group_ratio = heads_loc // kv_loc
        prefix_len = pre_dev * groups
        my_idx = lax.axis_index('cp')
        q_pos = block_positions(my_idx, groups, blk_len, prefix_len)
        cos_tab, sin_tab = rope_tables(q_pos, head_dim)
        hidden = rms_norm(x_loc, norm_attn)
        q_proj = jnp.dot(hidden, w_query, preferred_element_type=jnp.float32).reshape(rows_loc, heads_loc, head_dim)
        q_rot = apply_rope(q_proj, cos_tab, sin_tab).astype(jnp.bfloat16).reshape(rows_loc, kv_loc, group_ratio, head_dim)
        k_proj = jnp.dot(hidden, w_key, preferred_element_type=jnp.float32).reshape(rows_loc, kv_loc, head_dim)
        k_new = apply_rope(k_proj, cos_tab, sin_tab).astype(jnp.bfloat16)
        v_new = jnp.dot(hidden, w_value, preferred_element_type=jnp.float32).astype(jnp.bfloat16).reshape(rows_loc, kv_loc, head_dim)
        k_bundle = jnp.concatenate([kp_loc, k_new], axis=0)
        v_bundle = jnp.concatenate([vp_loc, v_new], axis=0)
        pre_offsets = jnp.arange(pre_dev, dtype=jnp.int32)

        def key_positions(src_idx):
            return jnp.concatenate([src_idx * pre_dev + pre_offsets, block_positions(src_idx, groups, blk_len, prefix_len)])

        score_scale = head_dim ** -0.5
        stat_shape = (rows_loc, kv_loc, group_ratio)
        init_state = (jnp.full(stat_shape, -jnp.inf, dtype=jnp.float32), jnp.zeros(stat_shape, jnp.float32), jnp.zeros(stat_shape + (head_dim,), jnp.float32))
        first_state = attend_step(init_state, q_rot, k_bundle, v_bundle, q_pos, key_positions(my_idx), score_scale)
        perm_pairs = [(dev_idx, (dev_idx + 1) % groups) for dev_idx in range(groups)]

        def step_body(step_idx, loop_state):
            k_cur, v_cur, acc_state = loop_state
            k_cur, v_cur = lax.ppermute((k_cur, v_cur), 'cp', perm_pairs)
            src_idx = (my_idx - step_idx) % groups
            acc_state = attend_step(acc_state, q_rot, k_cur, v_cur, q_pos, key_positions(src_idx), score_scale)
            return k_cur, v_cur, acc_state

        final_state = lax.fori_loop(1, groups, step_body, (k_bundle, v_bundle, first_state))[2]
        attn_heads = (final_state[2] / final_state[1][..., None]).astype(jnp.bfloat16).reshape(rows_loc, heads_loc * head_dim)
        resid_mid = x_loc.astype(jnp.float32) + lax.psum(jnp.dot(attn_heads, w_out, preferred_element_type=jnp.float32), 'tp')
        hidden_mlp = rms_norm(resid_mid, norm_mlp)
        gate_proj = jnp.dot(hidden_mlp, w_gate, preferred_element_type=jnp.float32)
        up_proj = jnp.dot(hidden_mlp, w_up, preferred_element_type=jnp.float32)
        act_mid = (jax.nn.silu(gate_proj) * up_proj).astype(jnp.bfloat16)
        x_out = (resid_mid + lax.psum(jnp.dot(act_mid, w_down, preferred_element_type=jnp.float32), 'tp')).astype(jnp.bfloat16)
        return x_out, k_new, v_new

    row_spec = P(('dp', 'cp'), None)
    kv_spec = P(('dp', 'cp'), 'tp', None)
    col_spec = P(None, 'tp')
    row_split = P('tp', None)
    vec_spec = P(None)
    return jax.shard_map(local_layer, mesh=mesh, in_specs=(row_spec, kv_spec, kv_spec, vec_spec, col_spec, col_spec, col_spec, row_split, vec_spec, col_spec, col_spec, row_split), out_specs=(row_spec, kv_spec, kv_spec), check_vma=False)
```

profile of v0, /device:TPU:97, one launch (start us, length us, event | category | flops | bytes accessed | tf_op | source)
XLA Modules:
  0.0 1258.7 jit_solution(11252479848966276642)
XLA Ops:
  11.1 4.2 fusion.27
  21.3 9.2 fusion.43
  40.8 21.4 %fusion.23 = (f32[1024,2,3]{0,2,1:T(4,128)S(1)}, f32[2,2048,1024,3]{2,1,3,0:T(8,128)}) fusion(pred[1024,2048]{0,1:T(8,128)(4,1)} %broadcast_compare_fusion.1, bf16[1024,2,3,128]{3,0,2,1:T(8,128)(2,1)S(1)} %copy-done.14, bf16[2048,2,128]{2,0,1:T(8,128)(2,1)} %maximum_maximum_fusion), kind=kOutput, calls=%fused_computation.32 | convolution fusion | flops 3258968064 | bytes 55074816 | tf_op jit(solution)/shard_map/sgrd,kgd->sgrk/dot_general | solution.py:39
  62.3 22.2 %fusion.22 = f32[1024,2,3]{0,2,1:T(4,128)S(1)} fusion(f32[2,2048,1024,3]{2,1,3,0:T(8,128)} %get-tuple-element.399, f32[1024,2,3]{0,2,1:T(4,128)S(1)} %get-tuple-element.472, pred[1024,2048]{0,1:T(8,128)(4,1)} %broadcast_compare_fusion.1), kind=kLoop, calls=%fused_computation.31 | loop fusion | flops 50325504 | bytes 52477952 | tf_op jit(solution)/shard_map/reduce_sum | solution.py:45
  84.6 5.4 convolution_convert_fusion
  90.5 22.4 %bitcast_add_fusion.1 = f32[1024,2,3,128]{0,3,2,1:T(8,128)} fusion(f32[2,2048,1024,3]{2,1,3,0:T(8,128)} %get-tuple-element.399, f32[1024,2,3]{0,2,1:T(4,128)S(1)} %get-tuple-element.472, pred[1024,2048]{0,1:T(8,128)(4,1)} %broadcast_compare_fusion.1, f32[1024,2,3]{0,2,1:T(4,128)S(1)} %get-tuple-element.394, bf16[1024,2,128]{0,2,1:T(8,128)(2,1)S(1)} %bitcast.88, ...), kind=kOutput, calls=%fused_computation.46 | convolution fusion | flops 3274440704 | bytes 56672256 | tf_op jit(solution)/shard_map/sgrk,kgd->sgrd/dot_general | solution.py:46
  112.9 3.5 copy.55
  117.8 578.7 %while.26 = (s32[]{:T(128)}, bf16[2048,2,128]{2,0,1:T(8,128)(2,1)}, bf16[2048,2,128]{2,0,1:T(8,128)(2,1)}, f32[1024,2,3]{0,2,1:T(4,128)S(1)}, f32[1024,2,3]{0,2,...) while((s32[]{:T(128)}, bf16[2048,2,128]{2,0,1:T(8,128)(2,1)}, ...), condition=%wide.region_6.7_spmd.clone.clone, body=%wide.region_3.6_spmd.clone.clone.sunk | while | flops 6584570880 | bytes 182362512 | solution.py:89
  118.2 2.7 collective-permute-start
  123.3 9.3 collective-permute-done
  132.6 20.3 %fusion.73 = (f32[1024,2,3]{0,2,1:T(4,128)S(1)}, f32[2,2048,1024,3]{2,1,3,0:T(8,128)}) fusion(pred[1024,2048]{0,1:T(8,128)(4,1)} %broadcast_compare_fusion.3, bf16[1024,2,3,128]{3,0,2,1:T(8,128)(2,1)} %get-tuple-element.506, bf16[2048,2,128]{2,0,1:T(8,128)(2,1)S(1)} %collective-permute-done), kind=kOutput, calls=%fused_computation.6.clone.1 | convolution fusion | flops 3258968064 | bytes 55074816 | tf_op jit(solution)/shard_map/while/body/eval_jaxpr/sgrd,kgd->sgrk/dot_general | solution.py:39
  152.9 22.0 %fusion.74 = f32[1024,2,3]{0,2,1:T(4,128)S(1)} fusion(f32[2,2048,1024,3]{2,1,3,0:T(8,128)} %get-tuple-element.466, f32[1024,2,3]{0,2,1:T(4,128)S(1)} %max.14, pred[1024,2048]{0,1:T(8,128)(4,1)} %broadcast_compare_fusion.3), kind=kLoop, calls=%fused_computation.5.clone.1 | loop fusion | flops 50325504 | bytes 52477952 | tf_op jit(solution)/shard_map/while/body/eval_jaxpr/reduce_sum | solution.py:45
  177.0 23.9 %bitcast_add_fusion.3 = f32[1024,2,3,128]{3,0,2,1:T(8,128)} fusion(f32[1024,2,3,128]{3,0,2,1:T(8,128)} %get-tuple-element.489, f32[2,2048,1024,3]{2,1,3,0:T(8,128)} %get-tuple-element.466, f32[1024,2,3]{0,2,1:T(4,128)S(1)} %max.14, pred[1024,2048]{0,1:T(8,128)(4,1)} %broadcast_compare_fusion.3, f32[1024,2,3]{0,2,1:T(4,128)S(1)} %get-tuple-element.468, ...), kind=kOutput, calls=%fused_computation.10.clone.1 | convolution fusion | flops 3273129984 | bytes 59817984 | tf_op jit(solution)/shard_map/while/body/eval_jaxpr/sgrk,kgd->sgrd/dot_general | solution.py:46
  205.8 9.4 collective-permute-done
  215.2 20.3 %fusion.73 = (f32[1024,2,3]{0,2,1:T(4,128)S(1)}, f32[2,2048,1024,3]{2,1,3,0:T(8,128)}) fusion(pred[1024,2048]{0,1:T(8,128)(4,1)} %broadcast_compare_fusion.3, bf16[1024,2,3,128]{3,0,2,1:T(8,128)(2,1)} %get-tuple-element.506, bf16[2048,2,128]{2,0,1:T(8,128)(2,1)S(1)} %collective-permute-done), kind=kOutput, calls=%fused_computation.6.clone.1 | convolution fusion | flops 3258968064 | bytes 55074816 | tf_op jit(solution)/shard_map/while/body/eval_jaxpr/sgrd,kgd->sgrk/dot_general | solution.py:39
  235.5 22.0 %fusion.74 = f32[1024,2,3]{0,2,1:T(4,128)S(1)} fusion(f32[2,2048,1024,3]{2,1,3,0:T(8,128)} %get-tuple-element.466, f32[1024,2,3]{0,2,1:T(4,128)S(1)} %max.14, pred[1024,2048]{0,1:T(8,128)(4,1)} %broadcast_compare_fusion.3), kind=kLoop, calls=%fused_computation.5.clone.1 | loop fusion | flops 50325504 | bytes 52477952 | tf_op jit(solution)/shard_map/while/body/eval_jaxpr/reduce_sum | solution.py:45
  259.6 23.9 %bitcast_add_fusion.3 = f32[1024,2,3,128]{3,0,2,1:T(8,128)} fusion(f32[1024,2,3,128]{3,0,2,1:T(8,128)} %get-tuple-element.489, f32[2,2048,1024,3]{2,1,3,0:T(8,128)} %get-tuple-element.466, f32[1024,2,3]{0,2,1:T(4,128)S(1)} %max.14, pred[1024,2048]{0,1:T(8,128)(4,1)} %broadcast_compare_fusion.3, f32[1024,2,3]{0,2,1:T(4,128)S(1)} %get-tuple-element.468, ...), kind=kOutput, calls=%fused_computation.10.clone.1 | convolution fusion | flops 3273129984 | bytes 59817984 | tf_op jit(solution)/shard_map/while/body/eval_jaxpr/sgrk,kgd->sgrd/dot_general | solution.py:46
  283.5 2.5 collective-permute-start
  288.4 9.4 collective-permute-done
  297.8 20.3 %fusion.73 = (f32[1024,2,3]{0,2,1:T(4,128)S(1)}, f32[2,2048,1024,3]{2,1,3,0:T(8,128)}) fusion(pred[1024,2048]{0,1:T(8,128)(4,1)} %broadcast_compare_fusion.3, bf16[1024,2,3,128]{3,0,2,1:T(8,128)(2,1)} %get-tuple-element.506, bf16[2048,2,128]{2,0,1:T(8,128)(2,1)S(1)} %collective-permute-done), kind=kOutput, calls=%fused_computation.6.clone.1 | convolution fusion | flops 3258968064 | bytes 55074816 | tf_op jit(solution)/shard_map/while/body/eval_jaxpr/sgrd,kgd->sgrk/dot_general | solution.py:39
  318.1 22.0 %fusion.74 = f32[1024,2,3]{0,2,1:T(4,128)S(1)} fusion(f32[2,2048,1024,3]{2,1,3,0:T(8,128)} %get-tuple-element.466, f32[1024,2,3]{0,2,1:T(4,128)S(1)} %max.14, pred[1024,2048]{0,1:T(8,128)(4,1)} %broadcast_compare_fusion.3), kind=kLoop, calls=%fused_computation.5.clone.1 | loop fusion | flops 50325504 | bytes 52477952 | tf_op jit(solution)/shard_map/while/body/eval_jaxpr/reduce_sum | solution.py:45
  342.2 23.9 %bitcast_add_fusion.3 = f32[1024,2,3,128]{3,0,2,1:T(8,128)} fusion(f32[1024,2,3,128]{3,0,2,1:T(8,128)} %get-tuple-element.489, f32[2,2048,1024,3]{2,1,3,0:T(8,128)} %get-tuple-element.466, f32[1024,2,3]{0,2,1:T(4,128)S(1)} %max.14, pred[1024,2048]{0,1:T(8,128)(4,1)} %broadcast_compare_fusion.3, f32[1024,2,3]{0,2,1:T(4,128)S(1)} %get-tuple-element.468, ...), kind=kOutput, calls=%fused_computation.10.clone.1 | convolution fusion | flops 3273129984 | bytes 59817984 | tf_op jit(solution)/shard_map/while/body/eval_jaxpr/sgrk,kgd->sgrd/dot_general | solution.py:46
  371.0 9.4 collective-permute-done
  380.3 20.3 %fusion.73 = (f32[1024,2,3]{0,2,1:T(4,128)S(1)}, f32[2,2048,1024,3]{2,1,3,0:T(8,128)}) fusion(pred[1024,2048]{0,1:T(8,128)(4,1)} %broadcast_compare_fusion.3, bf16[1024,2,3,128]{3,0,2,1:T(8,128)(2,1)} %get-tuple-element.506, bf16[2048,2,128]{2,0,1:T(8,128)(2,1)S(1)} %collective-permute-done), kind=kOutput, calls=%fused_computation.6.clone.1 | convolution fusion | flops 3258968064 | bytes 55074816 | tf_op jit(solution)/shard_map/while/body/eval_jaxpr/sgrd,kgd->sgrk/dot_general | solution.py:39
  400.7 22.0 %fusion.74 = f32[1024,2,3]{0,2,1:T(4,128)S(1)} fusion(f32[2,2048,1024,3]{2,1,3,0:T(8,128)} %get-tuple-element.466, f32[1024,2,3]{0,2,1:T(4,128)S(1)} %max.14, pred[1024,2048]{0,1:T(8,128)(4,1)} %broadcast_compare_fusion.3), kind=kLoop, calls=%fused_computation.5.clone.1 | loop fusion | flops 50325504 | bytes 52477952 | tf_op jit(solution)/shard_map/while/body/eval_jaxpr/reduce_sum | solution.py:45
  424.8 23.9 %bitcast_add_fusion.3 = f32[1024,2,3,128]{3,0,2,1:T(8,128)} fusion(f32[1024,2,3,128]{3,0,2,1:T(8,128)} %get-tuple-element.489, f32[2,2048,1024,3]{2,1,3,0:T(8,128)} %get-tuple-element.466, f32[1024,2,3]{0,2,1:T(4,128)S(1)} %max.14, pred[1024,2048]{0,1:T(8,128)(4,1)} %broadcast_compare_fusion.3, f32[1024,2,3]{0,2,1:T(4,128)S(1)} %get-tuple-element.468, ...), kind=kOutput, calls=%fused_computation.10.clone.1 | convolution fusion | flops 3273129984 | bytes 59817984 | tf_op jit(solution)/shard_map/while/body/eval_jaxpr/sgrk,kgd->sgrd/dot_general | solution.py:46
  453.6 9.4 collective-permute-done
  462.9 20.3 %fusion.73 = (f32[1024,2,3]{0,2,1:T(4,128)S(1)}, f32[2,2048,1024,3]{2,1,3,0:T(8,128)}) fusion(pred[1024,2048]{0,1:T(8,128)(4,1)} %broadcast_compare_fusion.3, bf16[1024,2,3,128]{3,0,2,1:T(8,128)(2,1)} %get-tuple-element.506, bf16[2048,2,128]{2,0,1:T(8,128)(2,1)S(1)} %collective-permute-done), kind=kOutput, calls=%fused_computation.6.clone.1 | convolution fusion | flops 3258968064 | bytes 55074816 | tf_op jit(solution)/shard_map/while/body/eval_jaxpr/sgrd,kgd->sgrk/dot_general | solution.py:39
  483.3 22.0 %fusion.74 = f32[1024,2,3]{0,2,1:T(4,128)S(1)} fusion(f32[2,2048,1024,3]{2,1,3,0:T(8,128)} %get-tuple-element.466, f32[1024,2,3]{0,2,1:T(4,128)S(1)} %max.14, pred[1024,2048]{0,1:T(8,128)(4,1)} %broadcast_compare_fusion.3), kind=kLoop, calls=%fused_computation.5.clone.1 | loop fusion | flops 50325504 | bytes 52477952 | tf_op jit(solution)/shard_map/while/body/eval_jaxpr/reduce_sum | solution.py:45
  507.4 23.9 %bitcast_add_fusion.3 = f32[1024,2,3,128]{3,0,2,1:T(8,128)} fusion(f32[1024,2,3,128]{3,0,2,1:T(8,128)} %get-tuple-element.489, f32[2,2048,1024,3]{2,1,3,0:T(8,128)} %get-tuple-element.466, f32[1024,2,3]{0,2,1:T(4,128)S(1)} %max.14, pred[1024,2048]{0,1:T(8,128)(4,1)} %broadcast_compare_fusion.3, f32[1024,2,3]{0,2,1:T(4,128)S(1)} %get-tuple-element.468, ...), kind=kOutput, calls=%fused_computation.10.clone.1 | convolution fusion | flops 3273129984 | bytes 59817984 | tf_op jit(solution)/shard_map/while/body/eval_jaxpr/sgrk,kgd->sgrd/dot_general | solution.py:46
  536.1 9.4 collective-permute-done
  545.5 20.3 %fusion.73 = (f32[1024,2,3]{0,2,1:T(4,128)S(1)}, f32[2,2048,1024,3]{2,1,3,0:T(8,128)}) fusion(pred[1024,2048]{0,1:T(8,128)(4,1)} %broadcast_compare_fusion.3, bf16[1024,2,3,128]{3,0,2,1:T(8,128)(2,1)} %get-tuple-element.506, bf16[2048,2,128]{2,0,1:T(8,128)(2,1)S(1)} %collective-permute-done), kind=kOutput, calls=%fused_computation.6.clone.1 | convolution fusion | flops 3258968064 | bytes 55074816 | tf_op jit(solution)/shard_map/while/body/eval_jaxpr/sgrd,kgd->sgrk/dot_general | solution.py:39
  565.8 22.0 %fusion.74 = f32[1024,2,3]{0,2,1:T(4,128)S(1)} fusion(f32[2,2048,1024,3]{2,1,3,0:T(8,128)} %get-tuple-element.466, f32[1024,2,3]{0,2,1:T(4,128)S(1)} %max.14, pred[1024,2048]{0,1:T(8,128)(4,1)} %broadcast_compare_fusion.3), kind=kLoop, calls=%fused_computation.5.clone.1 | loop fusion | flops 50325504 | bytes 52477952 | tf_op jit(solution)/shard_map/while/body/eval_jaxpr/reduce_sum | solution.py:45
  590.0 23.9 %bitcast_add_fusion.3 = f32[1024,2,3,128]{3,0,2,1:T(8,128)} fusion(f32[1024,2,3,128]{3,0,2,1:T(8,128)} %get-tuple-element.489, f32[2,2048,1024,3]{2,1,3,0:T(8,128)} %get-tuple-element.466, f32[1024,2,3]{0,2,1:T(4,128)S(1)} %max.14, pred[1024,2048]{0,1:T(8,128)(4,1)} %broadcast_compare_fusion.3, f32[1024,2,3]{0,2,1:T(4,128)S(1)} %get-tuple-element.468, ...), kind=kOutput, calls=%fused_computation.10.clone.1 | convolution fusion | flops 3273129984 | bytes 59817984 | tf_op jit(solution)/shard_map/while/body/eval_jaxpr/sgrk,kgd->sgrd/dot_general | solution.py:46
  618.7 9.4 collective-permute-done
  628.1 20.3 %fusion.73 = (f32[1024,2,3]{0,2,1:T(4,128)S(1)}, f32[2,2048,1024,3]{2,1,3,0:T(8,128)}) fusion(pred[1024,2048]{0,1:T(8,128)(4,1)} %broadcast_compare_fusion.3, bf16[1024,2,3,128]{3,0,2,1:T(8,128)(2,1)} %get-tuple-element.506, bf16[2048,2,128]{2,0,1:T(8,128)(2,1)S(1)} %collective-permute-done), kind=kOutput, calls=%fused_computation.6.clone.1 | convolution fusion | flops 3258968064 | bytes 55074816 | tf_op jit(solution)/shard_map/while/body/eval_jaxpr/sgrd,kgd->sgrk/dot_general | solution.py:39
  648.4 22.0 %fusion.74 = f32[1024,2,3]{0,2,1:T(4,128)S(1)} fusion(f32[2,2048,1024,3]{2,1,3,0:T(8,128)} %get-tuple-element.466, f32[1024,2,3]{0,2,1:T(4,128)S(1)} %max.14, pred[1024,2048]{0,1:T(8,128)(4,1)} %broadcast_compare_fusion.3), kind=kLoop, calls=%fused_computation.5.clone.1 | loop fusion | flops 50325504 | bytes 52477952 | tf_op jit(solution)/shard_map/while/body/eval_jaxpr/reduce_sum | solution.py:45
  672.5 23.9 %bitcast_add_fusion.3 = f32[1024,2,3,128]{3,0,2,1:T(8,128)} fusion(f32[1024,2,3,128]{3,0,2,1:T(8,128)} %get-tuple-element.489, f32[2,2048,1024,3]{2,1,3,0:T(8,128)} %get-tuple-element.466, f32[1024,2,3]{0,2,1:T(4,128)S(1)} %max.14, pred[1024,2048]{0,1:T(8,128)(4,1)} %broadcast_compare_fusion.3, f32[1024,2,3]{0,2,1:T(4,128)S(1)} %get-tuple-element.468, ...), kind=kOutput, calls=%fused_computation.10.clone.1 | convolution fusion | flops 3273129984 | bytes 59817984 | tf_op jit(solution)/shard_map/while/body/eval_jaxpr/sgrk,kgd->sgrd/dot_general | solution.py:46
  696.4 3.5 copy.56
  702.3 10.5 fusion.49
  713.5 231.4 %all-reduce.3.cloned.1.call-done = f32[1024,3072]{1,0:T(8,128)} async-done(((f32[1024,3072]{1,0:T(8,128)}), f32[1024,3072]{1,0:T(8,128)}) %all-reduce.3.cloned.1.call-update) | async-done | bytes 12582928 | tf_op jit(solution)/shard_map/psum | solution.py:91
  944.9 8.1 multiply_reduce_fusion
  953.0 7.7 multiply_convert_fusion
  960.7 16.2 %fusion.50 = f32[1024,2048]{1,0:T(8,128)S(1)} fusion(bf16[1024,3072]{1,0:T(8,128)(2,1)S(1)} %multiply_convert_fusion, bf16[3072,2048]{1,0:T(8,128)(2,1)} %param.23), kind=kOutput, calls=%fused_computation.83 | convolution fusion | flops 12884901888 | bytes 27262976 | tf_op jit(solution)/shard_map/dot_general | solution.py:93
  976.9 18.2 %multiply_convert_fusion.1 = bf16[1024,2048]{1,0:T(8,128)(2,1)} fusion(f32[1024,2048]{1,0:T(8,128)S(1)} %fusion.50, bf16[1024,3072]{1,0:T(8,128)(2,1)S(1)} %multiply_convert_fusion, bf16[3072,2048]{1,0:T(8,128)(2,1)} %param.24), kind=kOutput, calls=%fused_computation.44 | convolution fusion | flops 12897484800 | bytes 31457280 | tf_op jit(solution)/shard_map/dot_general | solution.py:94
  995.1 19.2 %fusion.51 = f32[1024,3072]{1,0:T(8,128)} fusion(bf16[1024,2048]{1,0:T(8,128)(2,1)} %multiply_convert_fusion.1, bf16[2048,3072]{1,0:T(8,128)(2,1)} %param.25), kind=kOutput, calls=%fused_computation.84 | convolution fusion | flops 12884901888 | bytes 29360128 | tf_op jit(solution)/shard_map/dot_general | solution.py:96
  1018.1 219.0 %all-reduce.5.cloned.1.call-done = f32[1024,3072]{1,0:T(8,128)} async-done(((f32[1024,3072]{1,0:T(8,128)}), f32[1024,3072]{1,0:T(8,128)}) %all-reduce.5.cloned.1.call-update) | async-done | bytes 12582928 | tf_op jit(solution)/shard_map/psum | solution.py:96
  1237.1 14.5 %add_convert_fusion = bf16[1024,3072]{1,0:T(8,128)(2,1)} fusion(f32[1024,3072]{1,0:T(8,128)} %all-reduce.5.cloned.1.call-done, f32[1024,3072]{1,0:T(8,128)} %all-reduce.3.cloned.1.call-done, bf16[1024,3072]{1,0:T(8,128)(2,1)} %param.14), kind=kLoop, calls=%fused_computation.41 | loop fusion | flops 12582912 | bytes 37748736 | tf_op jit(solution)/shard_map/convert_element_type | solution.py:96
  (153 shorter events, 72.3 us)
Async XLA Ops:
  7.2 8.2 copy-start
  7.2 937.7 %all-reduce.3.cloned.1.call-start = ((), (), s32[]{:S(2)}) async-start(), calls=%async_computation | async-start | bytes 25165824 | tf_op jit(solution)/shard_map/psum | solution.py:91
  10.3 5.1 copy-start.2
  15.4 5.0 copy-start.15
  34.6 4.5 copy-start.7
  34.6 4.5 copy-start.8
  34.6 4.4 copy-start.12
  34.6 4.4 copy-start.13
  34.6 4.7 copy-start.9
  39.0 1.8 copy-start.14
  39.3 22.9 %copy-start.3 = (bf16[1024,2,64]{2,0,1:T(8,128)(2,1)}, bf16[1024,2,64]{2,0,1:T(8,128)(2,1)S(1)}, u32[]{:S(2)}) copy-start(bf16[1024,2,64]{2,0,1:T(8,128)(2,1)S(1)} %get-tuple-element.390) | copy-start | bytes 786436
  39.3 22.9 %copy-start.5 = (bf16[1024,2,64]{2,0,1:T(8,128)(2,1)}, bf16[1024,2,64]{2,0,1:T(8,128)(2,1)S(1)}, u32[]{:S(2)}) copy-start(bf16[1024,2,64]{2,0,1:T(8,128)(2,1)S(1)} %get-tuple-element.391) | copy-start | bytes 786436
  84.6 5.4 copy-start.16
  90.0 22.9 %copy-start.10 = (bf16[1024,256]{0,1:T(8,128)(2,1)}, bf16[1024,256]{0,1:T(8,128)(2,1)S(1)}, u32[]{:S(2)}) copy-start(bf16[1024,256]{0,1:T(8,128)(2,1)S(1)} %convolution_convert_fusion) | copy-start | bytes 1572868
  118.2 14.4 %collective-permute-start = (bf16[2048,2,128]{2,0,1:T(8,128)(2,1)}, bf16[2048,2,128]{2,0,1:T(8,128)(2,1)S(1)}, u32[]{:S(2)}, u32[]{:S(2)}) collective-permute-start(bf16[2048,2,128]{2,0,1:T(8,128)(2,1)} %get-tuple-element.485), channel_id=1, source_target_pairs={{0,1},{1,2},{2,3},{3,4},{4,5},{5,6},{6,7},{7,0},{8,9},{9,10},{10,1... | collective-permute-start | bytes 3145736 | tf_op jit(solution)/shard_map/while/body/eval_jaxpr/ppermute | solution.py:84
  120.9 55.1 %collective-permute-start.1 = (bf16[2048,2,128]{2,0,1:T(8,128)(2,1)}, bf16[2048,2,128]{2,0,1:T(8,128)(2,1)S(1)}, u32[]{:S(2)}, u32[]{:S(2)}) collective-permute-start(bf16[2048,2,128]{2,0,1:T(8,128)(2,1)} %get-tuple-element.486), channel_id=1, source_target_pairs={{0,1},{1,2},{2,3},{3,4},{4,5},{5,6},{6,7},{7,0},{8,9},{9,10},{10,1... | collective-permute-start | bytes 3145736 | tf_op jit(solution)/shard_map/while/body/eval_jaxpr/ppermute | solution.py:84
  200.9 14.2 %collective-permute-start = (bf16[2048,2,128]{2,0,1:T(8,128)(2,1)}, bf16[2048,2,128]{2,0,1:T(8,128)(2,1)S(1)}, u32[]{:S(2)}, u32[]{:S(2)}) collective-permute-start(bf16[2048,2,128]{2,0,1:T(8,128)(2,1)} %get-tuple-element.485), channel_id=1, source_target_pairs={{0,1},{1,2},{2,3},{3,4},{4,5},{5,6},{6,7},{7,0},{8,9},{9,10},{10,1... | collective-permute-start | bytes 3145736 | tf_op jit(solution)/shard_map/while/body/eval_jaxpr/ppermute | solution.py:84
  203.4 55.1 %collective-permute-start.1 = (bf16[2048,2,128]{2,0,1:T(8,128)(2,1)}, bf16[2048,2,128]{2,0,1:T(8,128)(2,1)S(1)}, u32[]{:S(2)}, u32[]{:S(2)}) collective-permute-start(bf16[2048,2,128]{2,0,1:T(8,128)(2,1)} %get-tuple-element.486), channel_id=1, source_target_pairs={{0,1},{1,2},{2,3},{3,4},{4,5},{5,6},{6,7},{7,0},{8,9},{9,10},{10,1... | collective-permute-start | bytes 3145736 | tf_op jit(solution)/shard_map/while/body/eval_jaxpr/ppermute | solution.py:84
  283.5 14.3 %collective-permute-start = (bf16[2048,2,128]{2,0,1:T(8,128)(2,1)}, bf16[2048,2,128]{2,0,1:T(8,128)(2,1)S(1)}, u32[]{:S(2)}, u32[]{:S(2)}) collective-permute-start(bf16[2048,2,128]{2,0,1:T(8,128)(2,1)} %get-tuple-element.485), channel_id=1, source_target_pairs={{0,1},{1,2},{2,3},{3,4},{4,5},{5,6},{6,7},{7,0},{8,9},{9,10},{10,1... | collective-permute-start | bytes 3145736 | tf_op jit(solution)/shard_map/while/body/eval_jaxpr/ppermute | solution.py:84
  286.0 55.1 %collective-permute-start.1 = (bf16[2048,2,128]{2,0,1:T(8,128)(2,1)}, bf16[2048,2,128]{2,0,1:T(8,128)(2,1)S(1)}, u32[]{:S(2)}, u32[]{:S(2)}) collective-permute-start(bf16[2048,2,128]{2,0,1:T(8,128)(2,1)} %get-tuple-element.486), channel_id=1, source_target_pairs={{0,1},{1,2},{2,3},{3,4},{4,5},{5,6},{6,7},{7,0},{8,9},{9,10},{10,1... | collective-permute-start | bytes 3145736 | tf_op jit(solution)/shard_map/while/body/eval_jaxpr/ppermute | solution.py:84
  366.1 14.3 %collective-permute-start = (bf16[2048,2,128]{2,0,1:T(8,128)(2,1)}, bf16[2048,2,128]{2,0,1:T(8,128)(2,1)S(1)}, u32[]{:S(2)}, u32[]{:S(2)}) collective-permute-start(bf16[2048,2,128]{2,0,1:T(8,128)(2,1)} %get-tuple-element.485), channel_id=1, source_target_pairs={{0,1},{1,2},{2,3},{3,4},{4,5},{5,6},{6,7},{7,0},{8,9},{9,10},{10,1... | collective-permute-start | bytes 3145736 | tf_op jit(solution)/shard_map/while/body/eval_jaxpr/ppermute | solution.py:84
  368.6 55.1 %collective-permute-start.1 = (bf16[2048,2,128]{2,0,1:T(8,128)(2,1)}, bf16[2048,2,128]{2,0,1:T(8,128)(2,1)S(1)}, u32[]{:S(2)}, u32[]{:S(2)}) collective-permute-start(bf16[2048,2,128]{2,0,1:T(8,128)(2,1)} %get-tuple-element.486), channel_id=1, source_target_pairs={{0,1},{1,2},{2,3},{3,4},{4,5},{5,6},{6,7},{7,0},{8,9},{9,10},{10,1... | collective-permute-start | bytes 3145736 | tf_op jit(solution)/shard_map/while/body/eval_jaxpr/ppermute | solution.py:84
  448.7 14.3 %collective-permute-start = (bf16[2048,2,128]{2,0,1:T(8,128)(2,1)}, bf16[2048,2,128]{2,0,1:T(8,128)(2,1)S(1)}, u32[]{:S(2)}, u32[]{:S(2)}) collective-permute-start(bf16[2048,2,128]{2,0,1:T(8,128)(2,1)} %get-tuple-element.485), channel_id=1, source_target_pairs={{0,1},{1,2},{2,3},{3,4},{4,5},{5,6},{6,7},{7,0},{8,9},{9,10},{10,1... | collective-permute-start | bytes 3145736 | tf_op jit(solution)/shard_map/while/body/eval_jaxpr/ppermute | solution.py:84
  451.2 55.1 %collective-permute-start.1 = (bf16[2048,2,128]{2,0,1:T(8,128)(2,1)}, bf16[2048,2,128]{2,0,1:T(8,128)(2,1)S(1)}, u32[]{:S(2)}, u32[]{:S(2)}) collective-permute-start(bf16[2048,2,128]{2,0,1:T(8,128)(2,1)} %get-tuple-element.486), channel_id=1, source_target_pairs={{0,1},{1,2},{2,3},{3,4},{4,5},{5,6},{6,7},{7,0},{8,9},{9,10},{10,1... | collective-permute-start | bytes 3145736 | tf_op jit(solution)/shard_map/while/body/eval_jaxpr/ppermute | solution.py:84
  531.3 14.3 %collective-permute-start = (bf16[2048,2,128]{2,0,1:T(8,128)(2,1)}, bf16[2048,2,128]{2,0,1:T(8,128)(2,1)S(1)}, u32[]{:S(2)}, u32[]{:S(2)}) collective-permute-start(bf16[2048,2,128]{2,0,1:T(8,128)(2,1)} %get-tuple-element.485), channel_id=1, source_target_pairs={{0,1},{1,2},{2,3},{3,4},{4,5},{5,6},{6,7},{7,0},{8,9},{9,10},{10,1... | collective-permute-start | bytes 3145736 | tf_op jit(solution)/shard_map/while/body/eval_jaxpr/ppermute | solution.py:84
  533.8 55.1 %collective-permute-start.1 = (bf16[2048,2,128]{2,0,1:T(8,128)(2,1)}, bf16[2048,2,128]{2,0,1:T(8,128)(2,1)S(1)}, u32[]{:S(2)}, u32[]{:S(2)}) collective-permute-start(bf16[2048,2,128]{2,0,1:T(8,128)(2,1)} %get-tuple-element.486), channel_id=1, source_target_pairs={{0,1},{1,2},{2,3},{3,4},{4,5},{5,6},{6,7},{7,0},{8,9},{9,10},{10,1... | collective-permute-start | bytes 3145736 | tf_op jit(solution)/shard_map/while/body/eval_jaxpr/ppermute | solution.py:84
  613.8 14.3 %collective-permute-start = (bf16[2048,2,128]{2,0,1:T(8,128)(2,1)}, bf16[2048,2,128]{2,0,1:T(8,128)(2,1)S(1)}, u32[]{:S(2)}, u32[]{:S(2)}) collective-permute-start(bf16[2048,2,128]{2,0,1:T(8,128)(2,1)} %get-tuple-element.485), channel_id=1, source_target_pairs={{0,1},{1,2},{2,3},{3,4},{4,5},{5,6},{6,7},{7,0},{8,9},{9,10},{10,1... | collective-permute-start | bytes 3145736 | tf_op jit(solution)/shard_map/while/body/eval_jaxpr/ppermute | solution.py:84
  616.4 55.1 %collective-permute-start.1 = (bf16[2048,2,128]{2,0,1:T(8,128)(2,1)}, bf16[2048,2,128]{2,0,1:T(8,128)(2,1)S(1)}, u32[]{:S(2)}, u32[]{:S(2)}) collective-permute-start(bf16[2048,2,128]{2,0,1:T(8,128)(2,1)} %get-tuple-element.486), channel_id=1, source_target_pairs={{0,1},{1,2},{2,3},{3,4},{4,5},{5,6},{6,7},{7,0},{8,9},{9,10},{10,1... | collective-permute-start | bytes 3145736 | tf_op jit(solution)/shard_map/while/body/eval_jaxpr/ppermute | solution.py:84
  712.8 0.7 copy-start.17
  712.8 524.3 %all-reduce.5.cloned.1.call-start = ((), (), s32[]{:S(2)}) async-start(), calls=%async_computation.1 | async-start | bytes 25165824 | tf_op jit(solution)/shard_map/psum | solution.py:96
  1014.3 1.0 copy-start.11
  1014.3 2.1 copy-start.4
  1014.3 2.1 copy-start.6
  1237.1 14.5 %copy-start.1 = (bf16[3072,256]{1,0:T(8,128)(2,1)S(1)}, bf16[3072,256]{1,0:T(8,128)(2,1)}, u32[]{:S(2)}) copy-start(bf16[3072,256]{1,0:T(8,128)(2,1)} %param.19) | copy-start | bytes 4718596
Sparse Core Ops, SparseCore 0:
  713.0 231.9 all-reduce.2
  1014.5 222.5 all-reduce.4
where the time goes:
time: 1260 us
  waiting for transfers between devices  516 us (41%)
  matrix products  434 us (34%)
  other arithmetic  240 us (19%)
  local copies, waits for them, and re-layouts  35.4 us (3%)
  starting transfers between devices  18.2 us (1%)
  between operations  14.6 us (1%)
    psum x1, waiting for transfers between devices, local_layer(): lax.psum(jnp.dot(attn_heads, w_out, preferred_element_type=jnp.float32),...  231 us
    psum x1, waiting for transfers between devices, local_layer(): lax.psum(jnp.dot(act_mid, w_down, preferred_element_type=jnp.float32), 'tp')  219 us
    dot_general x8, matrix products, attend_step(): jnp.einsum('sgrk,kgd->sgrd', weights.astype(jnp.bfloat16), v_blk, preferr...  190 us
    reduce_sum x8, other arithmetic, attend_step(): denom_sum = denom_sum * correction + jnp.sum(weights, axis=-1)  176 us
    dot_general x8, matrix products, attend_step(): jnp.einsum('sgrd,kgd->sgrk', q_rot, k_blk, preferred_element_type=jnp.flo...  164 us
    ppermute x14, waiting for transfers between devices, step_body(): k_cur, v_cur = lax.ppermute((k_cur, v_cur), 'cp', perm_pairs)  65.5 us
  transfers between devices with their start and end apart: 16, of which 9 were waited for; matrix products, arithmetic and copies ran while one was open for 26% of the time, Pallas kernels for 0%

commit v1 on v0

v1 whole, which is shorter than its diff:
```python
import jax
import jax.numpy as jnp
from jax import lax
from jax.experimental import pallas as pl
from jax.experimental.pallas import tpu as pltpu
from jax.sharding import PartitionSpec as P

ROPE_THETA = 500000.0
NORM_EPS = 1e-5
LOG2E = 1.4426950408889634
F32 = jnp.float32
BF16 = jnp.bfloat16
MESH = pl.DeviceIdType.MESH
LANES = 128
SUB = 8
TILE = 256
NORM_ROWS = 32
WIDE = 512
VMEM_LIMIT = 63 * 2**20
S_LIMIT, V_LIMIT = 60.0, 40.0
HBM = pl.BlockSpec(memory_space=pl.ANY)
VMEM = pl.BlockSpec(memory_space=pltpu.VMEM)
(KP, VP, KE, VE, KL, VL, QE, QL, OE, OL) = range(10)
(K_RIGHT, V_RIGHT, K_LEFT, V_LEFT, K_ON, V_ON) = range(6)
(P_OWN, P_SIB, EARLY, LATE) = range(4)
(UP, DOWN, ON_UP, ON_DOWN) = range(4)


def scoped(name):
    def deco(f):
        def g(*a):
            with jax.named_scope(name):
                return f(*a)

        return g

    return deco


def dma(*shape):
    return pltpu.SemaphoreType.DMA(shape)


def start(copies):
    for c in copies:
        c.start()


def span(at, size, unit=LANES):
    return pl.ds(pl.multiple_of(at, unit), size)


def both(v):
    return lax.rem(v, 2)


def fold_rows(values, op):
    rows, cols = values.shape
    return op(values.reshape(rows // SUB, SUB, cols), axis=0)


def rms(x):
    return x * lax.rsqrt(jnp.mean(x * x, axis=-1, keepdims=True) + NORM_EPS)


def loop(n, body):
    lax.fori_loop(0, n, lambda i, c: (body(i), c)[1], 0)


def remote(src, dst, sems, i, who):
    send, recv = sems
    return pltpu.make_async_remote_copy(src_ref=src, dst_ref=dst, send_sem=send.at[i], recv_sem=recv.at[i], device_id=who, device_id_type=MESH)


def gather_steps(at, sems, ranks, src=None):
    here, up, down, over, size = ranks
    half = size // 2
    to_up, to_down = {"tp": up}, {"tp": down}

    def move(i, rank, first, n, who, other=None):
        ref = at(rank, first, n)
        return remote(ref if other is None else other, ref, sems, i, who)

    sends = [
        move(UP, here, 0, size, to_up, src),
        move(DOWN, here, 0, size, to_down, src),
        move(ON_UP, down, 0, half, to_up),
        move(ON_DOWN, up, half, half, to_down),
    ]
    brings = [
        move(UP, down, 0, size, to_up),
        move(DOWN, up, 0, size, to_down),
        move(ON_UP, over, 0, half, to_up),
        move(ON_DOWN, over, half, half, to_down),
    ]
    return sends, brings


def attention_call(exact, x_loc, kp2, vp2, cos_tab, sin_tab, norm_attn, w_query, w_key, w_value, w_out, groups, tps):
    rows, d = x_loc.shape
    blk = rows // 2
    hd = kp2.shape[1] // 2
    heads = w_query.shape[1] // hd
    ratio = heads // 2
    pre = kp2.shape[0]
    chips = groups // 2
    assert chips == tps == 4 and pre == rows and hd == LANES and ratio == 3
    deep = 2 * blk
    n_wide = heads * hd
    side = ratio * 2 * blk
    half_side = side // 2
    per_chip = 2 * pre
    suf = chips * per_chip
    send = suf + chips * 2 * rows
    send_pre = send + rows
    d_out = w_out.shape[1]
    w_half = d_out // 2
    w_rows = w_out.shape[0]
    scale = LOG2E * hd**-0.5
    n_proj = n_wide + 4 * hd

    def kernel(x_hbm, kp_hbm, vp_hbm, cos_ref, sin_ref, g_ref, wq_hbm, wk_hbm, wv_hbm, wo_hbm,
               k_out, v_out, oe_hbm, ol_hbm, wall_hbm, plain_out,
               w_buf, x_buf, h_0, h_1, q3, keys, vals, vp_buf, l_ref, a_ref, p_0, p_1, o_st, o_snd, size_all, size_tp, *rest):
        if exact:
            m_ref, s_0, s_1, t_0, t_1, c_0, c_1, *rest = rest
        l_sem, x_sem, sw_s, sw_r, x_s, x_r, w_s, w_r, d_s, d_r, o_s, o_r, z_s, z_r, y_s, y_r = rest
        me, t = lax.axis_index("cp"), lax.axis_index("tp")
        core, chip = both(me), lax.div(me, 2)
        sib = {"cp": me + 1 - 2 * core}
        x_right, x_left = {"cp": lax.rem(me + 2, groups)}, {"cp": lax.rem(me + groups - 2, groups)}
        up, down, over = [lax.rem(t + j, tps) for j in (1, tps - 1, 2)]

        def local(i, src, dst):
            return pltpu.make_async_copy(src, dst, l_sem.at[i])

        def x_copy(i):
            return pltpu.make_async_copy(x_hbm.at[span(i * TILE, TILE)], x_buf.at[both(i)], x_sem.at[both(i)])

        vp_copy = local(0, vp_hbm, vp_buf)
        kp_copy = local(1, kp_hbm.at[:, span(core * hd, hd)], keys.at[pl.ds(0, pre)])
        w_copies = [
            local(2, wq_hbm, w_buf.at[:, pl.ds(0, n_wide)]),
            local(3, wk_hbm, w_buf.at[:, pl.ds(n_wide, 2 * hd)]),
            local(4, wv_hbm, w_buf.at[:, pl.ds(n_wide + 2 * hd, 2 * hd)]),
        ]
        start([vp_copy, kp_copy, x_copy(0)] + w_copies + [x_copy(1)])

        greeted = [sib, x_right, x_left, {"tp": up}, {"tp": down}]
        if not exact:
            greeted = [{"cp": lax.rem(me + j, groups)} for j in range(1, groups)] + [{"tp": lax.rem(t + j, tps)} for j in range(1, tps)]
        barrier = pltpu.get_barrier_semaphore()
        for who in greeted:
            pl.semaphore_signal(barrier, inc=1, device_id=who, device_id_type=MESH)

        def w_place(which):
            return lambda rank, first, size: wall_hbm.at[span(rank * w_rows + first, size), span(which * w_half, w_half)]

        w_ranks = (t, up, down, over, w_rows)
        w_sends, w_brings = gather_steps(w_place(core), (w_s, w_r), w_ranks, wo_hbm.at[:, span(core * w_half, w_half)])
        w_theirs = gather_steps(w_place(1 - core), (d_s, d_r), w_ranks)[1]

        def w_share(i):
            ref = w_brings[i].dst_ref
            return remote(ref, ref, (d_s, d_r), i, sib)

        def o_cols(which):
            return span(which * ratio * hd, ratio * hd)

        def swap(i, arriving=False):
            if i == KP:
                src, dst = kp_hbm.at[:, span((1 - core) * hd, hd)], keys.at[pl.ds(pre, pre)]
            elif i == VP:
                src, dst = vals.at[pl.ds(send_pre, pre)], vals.at[pl.ds(pre, pre)]
            elif i in (KE, VE, KL, VL):
                buf, late = keys if i in (KE, KL) else vals, i in (KL, VL)
                src, dst = buf.at[pl.ds(send + late * blk, blk)], buf.at[pl.ds(suf + late * deep + blk, blk)]
            elif i in (QE, QL):
                at = pl.ds((i - QE) * half_side, half_side)
                src, dst = q3.at[2, :, at], q3.at[1, :, at]
            else:
                src, dst = o_snd.at[i - OE], o_st.at[i - OE, :, o_cols(1 - core if arriving else core)]
            return remote(src, dst, (sw_s, sw_r), i, sib)

        def region(item, slot):
            if item in (P_OWN, P_SIB):
                return pl.ds(slot * per_chip + item * pre, pre)
            return pl.ds(suf + (2 * slot + item - EARLY) * deep, deep)

        def ring(item):
            plan = {K_RIGHT: (keys, 0, 1, x_right), V_RIGHT: (vals, 0, 1, x_right), K_LEFT: (keys, 0, 3, x_left), V_LEFT: (vals, 0, 3, x_left),
                    K_ON: (keys, 1, 2, x_right), V_ON: (vals, 3, 2, x_left)}
            return [remote(buf.at[region(item, a)], buf.at[region(item, b)], (x_s.at[item], x_r.at[item]), i, who) for i, (buf, a, b, who) in plan.items()]

        @scoped("ring_on")
        def pass_on(item):
            got = ring(item)
            got[K_RIGHT].wait_recv()
            got[K_ON].start()
            got[V_LEFT].wait_recv()
            got[V_ON].start()

        @scoped("wait_sides")
        def sides_here(item):
            got = ring(item)
            got[V_RIGHT].wait_recv()
            got[K_LEFT].wait_recv()

        @scoped("wait_far")
        def far_here(item):
            got = ring(item)
            got[K_ON].wait_recv()
            got[V_ON].wait_recv()

        h_bufs = (h_0, h_1)

        def norm(i, slot):
            g = g_ref[...].astype(F32)[None, :]
            for r in range(0, TILE, NORM_ROWS):
                h_bufs[slot][r : r + NORM_ROWS, :] = (rms(x_buf[slot, r : r + NORM_ROWS, :].astype(F32)) * g).astype(BF16)

        if not exact:
            size_all[0] = jnp.zeros(size_all.shape[1:], F32)

        def note(i, v):
            if not exact:
                size_all[0, i : i + 1, :] = jnp.maximum(size_all[0, i : i + 1, :], v)

        def note_rows(i, v):
            if not exact:
                n2 = jnp.sum(v * v, axis=1, keepdims=True)
                note(i, jnp.broadcast_to(jnp.max(n2, axis=0, keepdims=True), (1, LANES)))

        def project(i, slot):
            h_tile = h_bufs[slot]
            late, sub = lax.div(i, blk // TILE), lax.rem(i, blk // TILE)
            at_rows = span(i * TILE, TILE)
            tab = span(sub * TILE, TILE)
            first = lax.broadcasted_iota(jnp.int32, (TILE, hd), 1) < hd // 2

            def table(ref):
                v = ref[tab, :]
                w = pltpu.roll(v, hd // 2, 1)
                return jnp.where(first == (late == 0), v, w)

            cos, sin = table(cos_ref), table(sin_ref)
            sin = jnp.where(first, -sin, sin)

            def rope(v):
                return v * cos + pltpu.roll(v, hd // 2, 1) * sin

            for pair in range(0, n_proj, 2 * hd):
                out = jnp.dot(h_tile[...], w_buf[:, pair : pair + 2 * hd], preferred_element_type=F32)
                for hh in range(2):
                    v = out[:, hh * hd : (hh + 1) * hd]
                    head = pair // hd + hh
                    lanes = pl.ds(hh * hd, hd)
                    at = jnp.where(core == hh, suf + late * deep, send + late * blk) + sub * TILE
                    if head < heads:
                        q_t = rope(v).astype(BF16).astype(F32).T
                        if not exact:
                            n2 = jnp.max(jnp.sum(fold_rows(q_t * q_t, jnp.sum), axis=0, keepdims=True), axis=1, keepdims=True)
                            note(0, jnp.broadcast_to(n2, (1, LANES)))
                        q_t = q_t * scale
                        hi = q_t.astype(BF16)
                        idx = jnp.where(core == head // ratio, 0, 2)
                        col = span(late * half_side + (head % ratio) * blk + sub * TILE, TILE)
                        q3[idx, pl.ds(0, hd), col] = hi
                        q3[idx, pl.ds(hd, hd), col] = (q_t - hi.astype(F32)).astype(BF16)
                    elif head < heads + 2:
                        k = rope(v).astype(BF16)
                        k_out[at_rows, lanes] = k
                        keys[span(at, TILE), :] = k
                        note_rows(1, k.astype(F32))
                    else:
                        v = v.astype(BF16)
                        v_out[at_rows, lanes] = v
                        v_t = v.astype(F32).T
                        if not exact:
                            note(2, jnp.max(fold_rows(jnp.abs(v.astype(F32)), jnp.max), axis=0, keepdims=True))
                        for b in range(0, TILE, LANES):
                            vals[span(at + b, LANES), :] = v_t[:, b : b + LANES].astype(BF16)

        vp_copy.wait()
        for j in range(2):
            at = jnp.where(core == j, 0, send_pre)
            for b in range(0, pre, LANES):
                v = vp_buf[b : b + LANES, j * hd : (j + 1) * hd].astype(F32)
                vals[span(at + b, LANES), :] = v.T.astype(BF16)
        x_copy(0).wait()
        norm(0, 0)
        kp_copy.wait()
        pl.semaphore_wait(barrier, len(greeted))
        start([swap(KP), swap(VP)] + ring(P_OWN)[:K_ON] + w_sends[:ON_UP])
        if not exact:
            for r in range(0, pre, TILE):
                note(2, jnp.max(fold_rows(jnp.maximum(*[jnp.abs(vp_buf[r : r + TILE, j * hd : (j + 1) * hd].astype(F32)) for j in range(2)]), jnp.max), axis=0, keepdims=True))
                note_rows(1, keys[r : r + TILE, :].astype(F32))
        with jax.named_scope("w_wait"):
            for c in w_copies:
                c.wait()

        n_tiles = rows // TILE

        @scoped("project")
        def two_tiles(j):
            i = 2 * j
            x_copy(i + 1).wait()

            @pl.when(i + 2 < n_tiles)
            def _():
                x_copy(i + 2).start()

            norm(i + 1, 1)
            project(i, 0)

            @pl.when(j == 0)
            def _():
                swap(KP).wait_recv()
                swap(VP).wait_recv()
                start(ring(P_SIB)[:K_ON])

            @pl.when(i + 2 < n_tiles)
            def _():
                x_copy(i + 3).start()
                x_copy(i + 2).wait()

            norm(i + 2, 0)
            project(i + 1, 1)

            @pl.when(j == 0)
            def _():
                start([swap(i) for i in (KE, VE, QE)])

        loop(n_tiles // 2, two_tiles)
        start([swap(i) for i in (KL, VL, QL)])

        def size_copies():
            out = []
            for j in range(1, groups):
                out.append(remote(size_all.at[0], size_all.at[j], (z_s, z_r), j, {"cp": lax.rem(me + j, groups)}))
            return out

        def size_on():
            return [remote(size_tp.at[0], size_tp.at[j], (y_s, y_r), j, {"tp": lax.rem(t + j, tps)}) for j in range(1, tps)]

        def sizes_meet():
            for c in size_copies():
                c.wait_recv()
            size_tp[0] = jnp.max(size_all[...], axis=0)
            start(size_on())

        if not exact:
            start(size_copies())
        if exact:
            m_ref[...] = jnp.full_like(m_ref, -jnp.inf)
        l_ref[...] = jnp.zeros_like(l_ref)
        a_ref[...] = jnp.zeros_like(a_ref)
        with jax.named_scope("swap_wait"):
            for i in range(KE, OE):
                swap(i).wait_recv()

        p_bufs = (p_0, p_1)
        if exact:
            s_bufs, t_bufs, c_bufs = (s_0, s_1), (t_0, t_1), (c_0, c_1)
        part = TILE
        lead = 2 if exact else 1
        unroll = 2 if exact else 4

        def state_at(step):
            who, late, head = step[:3]
            return span(who * side + late * half_side + head * blk, blk)

        def scores(step, slot, shifts):
            who, late, head, key = step
            q = q3[who, :, span(late * half_side + head * blk, blk)]
            cols = state_at(step)
            top = None
            for r in range(0, deep, part):
                k = keys[span(key + r, part), :]
                s = jnp.dot(jnp.concatenate([k, k], axis=1), q, preferred_element_type=F32)
                if shifts is not None:
                    row = lax.broadcasted_iota(jnp.int32, s.shape, 0) + r % blk
                    col = lax.broadcasted_iota(jnp.int32, s.shape, 1) + shifts[r // blk]
                    s = jnp.where(row <= col, s, -jnp.inf)
                if exact:
                    s_bufs[slot][r : r + part, :] = s
                    t8 = fold_rows(s, jnp.max)
                    top = t8 if top is None else jnp.maximum(top, t8)
                else:
                    p = jnp.exp2(s)
                    p_bufs[slot][r : r + part, :] = p.astype(BF16)
                    t8 = fold_rows(p, jnp.sum)
                    top = t8 if top is None else top + t8
            if exact:
                t_bufs[slot][...] = top
            else:
                l_ref[:, cols] += top

        def softmax(step, slot):
            cols = state_at(step)
            m_old = m_ref[:, cols]
            m_new = jnp.maximum(m_old, jnp.max(t_bufs[slot][...], axis=0, keepdims=True))
            corr = jnp.exp2(m_old - m_new)
            total = None
            for r in range(0, deep, part):
                p = jnp.exp2(s_bufs[slot][r : r + part, :] - m_new)
                t8 = fold_rows(p, jnp.sum)
                total = t8 if total is None else total + t8
                p_bufs[slot][r : r + part, :] = p.astype(BF16)
            l_ref[:, cols] = l_ref[:, cols] * corr + total
            m_ref[:, cols] = m_new
            c_bufs[slot][...] = corr

        def values(step, slot):
            cols, key = state_at(step), step[3]
            v = jnp.concatenate([vals[span(key + b, LANES), :] for b in range(0, deep, LANES)], axis=1)
            pv = jnp.dot(v, p_bufs[slot][...], preferred_element_type=F32)
            a_ref[:, cols] = a_ref[:, cols] * c_bufs[slot][...] + pv if exact else a_ref[:, cols] + pv

        def run(n_steps, where, service, mask=None):
            def sc(u, slot):
                scores(where(u), slot, None if mask is None else mask(where(u)))

            def sm(u, slot):
                if exact:
                    softmax(where(u), slot)

            for u in range(lead):
                sc(u, u)
            sm(0, 0)
            slot = lambda u: u % 2

            @scoped("body")
            def body(i):
                service(i)
                for u in range(unroll):
                    sc(unroll * i + u + lead, slot(u + lead))
                    sm(unroll * i + u + 1, slot(u + 1))
                    values(where(unroll * i + u), slot(u))

            trips = (n_steps - lead) // unroll
            loop(trips, body)
            for u in range(unroll * trips, n_steps):
                if u + lead < n_steps:
                    sc(u + lead, slot(u + lead))
                if u + 1 < n_steps:
                    sm(u + 1, slot(u + 1))
                values(where(u), slot(u))

        def own_where(u):
            who, rest = lax.div(u, 2 * ratio), lax.rem(u, 2 * ratio)
            late, head = lax.div(rest, ratio), lax.rem(rest, ratio)
            return who, late, head, suf + late * deep

        def own_mask(step):
            who, late = step[:2]
            q_core = jnp.where(who == 0, core, 1 - core)
            seen = jnp.where(late == 0, q_core, 1 - q_core)
            other = (2 * seen - 1) * blk
            return jnp.where(who == 0, 0, other), jnp.where(who == 0, other, 0)

        with jax.named_scope("run_own"):
            run(4 * ratio, own_where, lambda i: None, own_mask)

        qt = 2 * ratio
        pc = per_chip // deep
        n_sides, n_far = 2 * qt * pc, qt * pc
        b1 = 2 * qt * pc
        b2 = b1 + qt
        b3 = b2 + n_sides
        b4 = b3 + n_far
        b5 = b4 + qt * chip
        b7 = b5 + n_sides + n_far
        b8 = b7 + qt * (chips - 1)
        n_main = b4 + n_sides + n_far + 2 * qt * (chips - 1)

        def where(u):
            late = (u >= b5).astype(jnp.int32)
            v = u - jnp.where(u >= b5, b5 - b2, 0)
            j = v - b2
            q_i, r = lax.div(j, 2 * pc), lax.rem(j, 2 * pc)
            key = (1 + 2 * lax.div(r, pc)) * per_chip + lax.rem(r, pc) * deep
            j = v - b3
            q_i = jnp.where(v < b3, q_i, lax.div(j, pc))
            key = jnp.where(v < b3, key, 2 * per_chip + lax.rem(j, pc) * deep)
            j = u - b4
            here = (u >= b4) & (u < b5)
            q_i = jnp.where(here, lax.rem(j, qt), q_i)
            key = jnp.where(here, suf + (1 + lax.div(j, qt)) * 2 * deep, key)
            j = u - b7
            here = u >= b7
            q_i = jnp.where(here, lax.div(j, chips - 1), q_i)
            key = jnp.where(here, suf + (1 + lax.rem(j, chips - 1)) * 2 * deep, key)
            j = u - b8
            here = u >= b8
            q_i = jnp.where(here, lax.rem(j, qt), q_i)
            key = jnp.where(here, suf + (1 + chip + lax.div(j, qt)) * 2 * deep + deep, key)
            here = u < b2
            q_i = jnp.where(here, u - b1, q_i)
            key = jnp.where(here, suf, key)
            late = jnp.where(here, 1, late)
            tile = lax.div(u, pc)
            here = u < b1
            q_i = jnp.where(here, lax.rem(tile, qt), q_i)
            late = jnp.where(here, lax.div(tile, qt), late)
            key = jnp.where(here, lax.rem(u, pc) * deep, key)
            return lax.div(q_i, ratio), late, lax.rem(q_i, ratio), key

        @scoped("finalize")
        def finalize(h):
            for who in range(2):
                for head in range(ratio):
                    at = who * side + h * half_side + head * blk
                    inv = 1.0 / jnp.sum(l_ref[:, at : at + blk], axis=0, keepdims=True)
                    o = (a_ref[:, at : at + blk] * inv).T.astype(BF16)
                    if who == 0:
                        o_st[h, :, span(core * ratio * hd + head * hd, hd)] = o
                    else:
                        o_snd[h, :, pl.ds(head * hd, hd)] = o
            swap(OE + h).start()

        def o_place(rank, first, size):
            return oe_hbm.at[pl.ds(first, size), span(rank * n_wide, n_wide)]

        o_sends, o_brings = gather_steps(o_place, (o_s, o_r), (t, up, down, over, blk), o_st.at[0])

        def o_keep(h):
            return local(h, o_st.at[h], (oe_hbm, ol_hbm)[h].at[:, span(t * n_wide, n_wide)])

        def at_trip(events):
            def service(i):
                for when, what in events:
                    pl.when(i == when)(lambda what=what: (what(), None)[1])

            return service

        def suffix_early():
            pass_on(P_OWN)
            pass_on(P_SIB)
            start(ring(EARLY)[:K_ON])

        @scoped("svc_w")
        def suffix_late():
            pass_on(EARLY)
            start(ring(LATE)[:K_ON])
            for b in w_brings[:ON_UP]:
                b.wait_recv()
            start(w_sends[ON_UP:])
            start([w_share(UP), w_share(DOWN)])

        def early_suffix_here():
            sides_here(EARLY)
            far_here(EARLY)

        @scoped("svc_o")
        def early_o():
            swap(OE, True).wait_recv()
            start(o_sends[:ON_UP])
            o_keep(0).start()
            pass_on(LATE)

        @scoped("svc_o2")
        def early_o_on():
            for b in o_brings[:ON_UP]:
                b.wait_recv()
            start(o_sends[ON_UP:])
            for i in (ON_UP, ON_DOWN):
                w_brings[i].wait_recv()
                w_share(i).start()

        def late_suffix_here():
            sides_here(LATE)
            far_here(LATE)

        def trip(step):
            return lax.div(step - lead, unroll)

        e_done = lax.div(b5 + unroll - 1, unroll)
        trips = (n_main - lead) // unroll
        events = [
            (3, suffix_early),
            (trip(b2), lambda: [sides_here(P_OWN), sides_here(P_SIB)]),
            (trip(b3) - 2, suffix_late),
            (trip(b3), lambda: [far_here(P_OWN), far_here(P_SIB)]),
            (trip(b4), early_suffix_here),
            (e_done, lambda: finalize(0)),
            (e_done + 2, early_o),
            (e_done + 10, early_o_on),
            (trip(b8), late_suffix_here),
        ]
        if not exact:
            events.append((e_done + 4, sizes_meet))
        with jax.named_scope("run_main"):
            run(n_main, where, at_trip(events))

        pl.when(trip(b8) >= trips)(late_suffix_here)
        finalize(1)

        if exact:
            plain_out[0, 0] = 1
        else:
            for c in size_on():
                c.wait_recv()
            top = jnp.max(jnp.max(size_tp[...], axis=0), axis=1)
            fits = (scale * scale * top[0] * top[1] <= S_LIMIT**2) & (top[2] <= 2.0**V_LIMIT)
            plain_out[0, 0] = fits.astype(jnp.int32)
        with jax.named_scope("tail"):
            swap(OL, True).wait_recv()
            o_keep(1).start()
            for b in o_brings[ON_UP:] + w_theirs:
                b.wait_recv()
            for i in range(OL + 1):
                swap(i).wait_send()
            for item in (P_OWN, P_SIB, EARLY, LATE):
                for c in ring(item):
                    c.wait_send()
            for c in w_sends + [w_share(i) for i in range(4)] + o_sends:
                c.wait_send()
            if not exact:
                for c in size_copies() + size_on():
                    c.wait_send()
            o_keep(0).wait()
            o_keep(1).wait()

    n_state = 2 * side
    scratch = [
        pltpu.VMEM((d, n_proj), BF16),
        pltpu.VMEM((2, TILE, d), BF16),
        pltpu.VMEM((TILE, d), BF16),
        pltpu.VMEM((TILE, d), BF16),
        pltpu.VMEM((3, 2 * hd, side), BF16),
        pltpu.VMEM((send_pre, hd), BF16),
        pltpu.VMEM((send_pre + pre, hd), BF16),
        pltpu.VMEM((pre, 2 * hd), BF16),
        pltpu.VMEM((SUB, n_state), F32),
        pltpu.VMEM((hd, n_state), F32),
        pltpu.VMEM((deep, blk), BF16),
        pltpu.VMEM((deep, blk), BF16),
        pltpu.VMEM((2, blk, n_wide), BF16),
        pltpu.VMEM((2, blk, ratio * hd), BF16),
        pltpu.VMEM((groups, SUB, LANES), F32),
        pltpu.VMEM((tps, SUB, LANES), F32),
    ]
    if exact:
        scratch += [pltpu.VMEM((1, n_state), F32)]
        scratch += [pltpu.VMEM((deep, blk), F32)] * 2 + [pltpu.VMEM((SUB, blk), F32)] * 2 + [pltpu.VMEM((1, blk), F32)] * 2
    scratch += [dma(5), dma(2), dma(10), dma(10), dma(4, 6), dma(4, 6)] + [dma(4)] * 6 + [dma(groups)] * 2 + [dma(tps)] * 2
    shapes = [(rows, 2 * hd)] * 2 + [(blk, tps * n_wide)] * 2 + [(tps * w_rows, d_out)]
    return pl.pallas_call(
        kernel,
        in_specs=[HBM] * 3 + [VMEM] * 3 + [HBM] * 4,
        out_specs=[VMEM, VMEM, HBM, HBM, HBM, pl.BlockSpec(memory_space=pltpu.SMEM)],
        out_shape=[jax.ShapeDtypeStruct(s, BF16) for s in shapes] + [jax.ShapeDtypeStruct((1, 1), jnp.int32)],
        scratch_shapes=scratch,
        compiler_params=pltpu.CompilerParams(collective_id=2 + exact, has_side_effects=True, vmem_limit_bytes=VMEM_LIMIT),
        name="attention_exact" if exact else "attention",
    )(x_loc, kp2, vp2, cos_tab, sin_tab, norm_attn, w_query, w_key, w_value, w_out)


def mlp_call(x_loc, o_early, o_late, w_out, w_out_all, norm_mlp, w_gate, w_up, w_down, tps):
    rows, d = x_loc.shape
    blk, d_in = o_early.shape
    n_wide = d_in // tps
    ff = w_gate.shape[1]
    n_chunks = rows // TILE
    quarter = TILE // tps
    half = quarter // 2
    gate = WIDE // 2
    n_a, n_b, n_c = d // WIDE, ff // gate, d // WIDE
    per = n_a + n_b + n_c
    total = per * n_chunks
    slots = 3
    (FAR_R, FAR_L, NEAR_R, NEAR_L, SUM_R, SUM_L, OUT_R, OUT_L, ON_R, ON_L) = range(10)

    def kernel(x_hbm, oe_hbm, ol_in, wo_hbm, wall_hbm, g_ref, wg_hbm, wu_hbm, wd_hbm, out_hbm, ol_hbm,
               w_buf, o_buf, x_buf, y_buf, h_buf, act_buf, part, got1, got2, y_own, fin, w_sem, row_sem, c_s, c_r, c_sem, o_s, o_r):
        t = lax.axis_index("tp")
        right, left, far = [lax.rem(t + j, tps) for j in (1, tps - 1, 2)]

        def w_copies(kind, i, slot):
            def get(j, src, dst):
                return pltpu.make_async_copy(src, dst, w_sem.at[slot, j])

            if kind == 0:
                cols, out = span(i * WIDE, WIDE), []
                for j in range(tps):
                    at = span(lax.rem(t + j, tps) * n_wide, n_wide)
                    out.append(get(j, wo_hbm.at[:, cols] if j == 0 else wall_hbm.at[at, cols], w_buf.at[slot, at]))
                return out
            if kind == 1:
                at = span(i * gate, gate)
                return [get(j, w.at[:, at], w_buf.at[slot, :, pl.ds(j * gate, gate)]) for j, w in enumerate((wg_hbm, wu_hbm))]
            return [get(0, wd_hbm.at[:, span(i * WIDE, WIDE)], w_buf.at[slot, pl.ds(0, ff)])]

        def fetch(g):
            i, slot = lax.rem(g, per), lax.rem(g, slots)
            for kind, first, n in ((0, 0, n_a), (1, n_a, n_b), (2, n_a + n_b, n_c)):
                pl.when((g < total) & (i >= first) & (i < first + n))(lambda: start(w_copies(kind, i - first, slot)))

        def row_copies(c, slot, src):
            at = span(c * TILE, TILE)
            return [
                pltpu.make_async_copy(x_hbm.at[at], x_buf.at[slot], row_sem.at[0, slot]),
                pltpu.make_async_copy(src.at[span(lax.rem(c * TILE, blk), TILE)], o_buf.at[slot], row_sem.at[1, slot]),
            ]

        def start_rows(c, slot):
            pl.when(c < blk // TILE)(lambda: start(row_copies(c, slot, oe_hbm)))
            pl.when(c >= blk // TILE)(lambda: start(row_copies(c, slot, ol_hbm)))

        start(row_copies(0, 0, oe_hbm))
        fetch(0)
        fetch(1)
        greeted = [{"tp": who} for who in (right, left)]
        barrier = pltpu.get_barrier_semaphore()
        for who in greeted:
            pl.semaphore_signal(barrier, inc=1, device_id=who, device_id_type=MESH)
        pl.semaphore_wait(barrier, len(greeted))

        def ol_place(rank, first, n):
            return ol_hbm.at[pl.ds(first, n), span(rank * n_wide, n_wide)]

        o_sends, o_brings = gather_steps(ol_place, (o_s, o_r), (t, right, left, far, blk))
        start(o_sends[:ON_UP])

        def out_rows(c, q, first, n):
            return out_hbm.at[span(c * TILE + q * quarter + first, n, half)]

        def at_rows(q, first, n):
            return span(q * quarter + first, n, half)

        def moves(c):
            def go(i, src, dst):
                return remote(src, dst, (c_s.at[c], c_r.at[c]), i, {"tp": right if i % 2 == 0 else left})

            def mine(q, first):
                return part.at[c, at_rows(q, first, half)]

            top, low = pl.ds(0, half), pl.ds(half, half)
            sends = {
                FAR_R: (mine(far, 0), got1.at[c, 0]),
                FAR_L: (mine(far, half), got1.at[c, 1]),
                NEAR_R: (mine(right, half), got2.at[c, 0, low]),
                NEAR_L: (mine(left, 0), got2.at[c, 1, top]),
                SUM_R: (mine(right, 0), got2.at[c, 0, top]),
                SUM_L: (mine(left, half), got2.at[c, 1, low]),
                OUT_R: (fin.at[c], out_rows(c, t, 0, quarter)),
                OUT_L: (fin.at[c], out_rows(c, t, 0, quarter)),
                ON_R: (out_rows(c, left, 0, half), out_rows(c, left, 0, half)),
                ON_L: (out_rows(c, right, half, half), out_rows(c, right, half, half)),
            }
            brings = {
                OUT_R: (fin.at[c], out_rows(c, left, 0, quarter)),
                OUT_L: (fin.at[c], out_rows(c, right, 0, quarter)),
                ON_R: (out_rows(c, far, 0, half), out_rows(c, far, 0, half)),
                ON_L: (out_rows(c, far, half, half), out_rows(c, far, half, half)),
            }
            return [go(i, *s) for i, s in sends.items()], {i: go(i, *s) for i, s in brings.items()}

        def own_copy(c):
            return pltpu.make_async_copy(fin.at[c], out_rows(c, t, 0, quarter), c_sem.at[c])

        @scoped("middle")
        def middle(c):
            m = moves(c)[0]
            for way, q, first in ((0, right, 0), (1, left, half)):
                m[FAR_R + way].wait_recv()
                part[c, at_rows(q, first, half), :] += got1[c, way]
                m[SUM_R + way].start()

        @scoped("finish")
        def finish(c):
            m = moves(c)[0]
            for i in (NEAR_R, NEAR_L, SUM_R, SUM_L):
                m[i].wait_recv()
            fin[c] = (y_own[c] + (part[c, at_rows(t, 0, quarter), :] + (got2[c, 0] + got2[c, 1]))).astype(BF16)
            own_copy(c).start()
            start(m[OUT_R:ON_R])

        @scoped("forward")
        def forward(c):
            m, b = moves(c)
            for way in range(2):
                b[OUT_R + way].wait_recv()
                m[ON_R + way].start()

        @scoped("drain")
        def drain(c):
            m, b = moves(c)
            b[ON_R].wait_recv()
            b[ON_L].wait_recv()
            for s in m:
                s.wait_send()
            own_copy(c).wait()

        def tiles(n, base, kind, body):
            @scoped("tile_" + "abc"[kind])
            def one(i):
                g = base + i
                fetch(g + 2)
                slot = lax.rem(g, slots)
                for cp in w_copies(kind, i, slot):
                    cp.wait()
                body(i, slot)

            loop(n, one)

        def step(c):
            base = c * per
            row_slot = both(c)
            for cp in row_copies(0, row_slot, oe_hbm):
                cp.wait()

            def tile_a(i, slot):
                at = span(i * WIDE, WIDE)
                y_buf[:, at] = x_buf[row_slot, :, at].astype(F32) + jnp.dot(o_buf[row_slot], w_buf[slot], preferred_element_type=F32)

            tiles(n_a, base, 0, tile_a)
            y_own[c] = y_buf[span(t * quarter, quarter, quarter), :]

            def norm(i):
                at = span(i * NORM_ROWS, NORM_ROWS, NORM_ROWS)
                h_buf[at, :] = (rms(y_buf[at, :]) * g_ref[...].astype(F32)[None, :]).astype(BF16)

            loop(TILE // NORM_ROWS, norm)
            pl.when(c >= 1)(lambda: middle(c - 1))

            def tile_b(i, slot):
                pair = jnp.dot(h_buf[...], w_buf[slot], preferred_element_type=F32)
                act_buf[:, span(i * gate, gate)] = (jax.nn.silu(pair[:, :gate]) * pair[:, gate:]).astype(BF16)

            tiles(n_b, base + n_a, 1, tile_b)
            pl.when(c >= 2)(lambda: forward(c - 2))

            @pl.when(c == 0)
            def _():
                for b, s in zip(o_brings, o_sends[ON_UP:]):
                    b.wait_recv()
                    s.start()

            @pl.when(c == 1)
            def _():
                for b in o_brings[ON_UP:]:
                    b.wait_recv()

            pl.when(c + 1 < n_chunks)(lambda: start_rows(c + 1, 1 - row_slot))

            def tile_c(i, slot):
                part[c, :, span(i * WIDE, WIDE)] = jnp.dot(act_buf[...], w_buf[slot, 0:ff, :], preferred_element_type=F32)

            tiles(n_c, base + n_a + n_b, 2, tile_c)
            start(moves(c)[0][:SUM_R])
            pl.when(c >= 1)(lambda: finish(c - 1))

        loop(n_chunks, step)
        last = n_chunks - 1
        middle(last)
        forward(last - 1)
        finish(last)
        forward(last)
        loop(n_chunks, drain)
        for s in o_sends:
            s.wait_send()

    return pl.pallas_call(
        kernel,
        in_specs=[HBM] * 5 + [VMEM] + [HBM] * 3,
        out_specs=[HBM, HBM],
        out_shape=[jax.ShapeDtypeStruct((rows, d), BF16), jax.ShapeDtypeStruct(o_late.shape, BF16)],
        input_output_aliases={2: 1},
        scratch_shapes=[
            pltpu.VMEM((slots, d_in, WIDE), BF16),
            pltpu.VMEM((2, TILE, d_in), BF16),
            pltpu.VMEM((2, TILE, d), BF16),
            pltpu.VMEM((TILE, d), F32),
            pltpu.VMEM((TILE, d), BF16),
            pltpu.VMEM((TILE, ff), BF16),
            pltpu.VMEM((n_chunks, TILE, d), F32),
            pltpu.VMEM((n_chunks, 2, half, d), F32),
            pltpu.VMEM((n_chunks, 2, quarter, d), F32),
            pltpu.VMEM((n_chunks, quarter, d), F32),
            pltpu.VMEM((n_chunks, quarter, d), BF16),
            dma(slots, tps), dma(2, 2), dma(n_chunks, 10), dma(n_chunks, 10), dma(n_chunks), dma(4), dma(4),
        ],
        compiler_params=pltpu.CompilerParams(collective_id=4, has_side_effects=True, vmem_limit_bytes=VMEM_LIMIT),
        name="mlp",
    )(x_loc, o_early, o_late, w_out, w_out_all, norm_mlp, w_gate, w_up, w_down)


def angle_tables(owner, groups, blk, prefix_len, hd):
    lane = jnp.arange(hd, dtype=jnp.int32)
    early = lane < hd // 2
    block = jnp.where(early, owner, 2 * groups - 1 - owner)
    pos = prefix_len + block[None, :] * blk + jnp.arange(blk, dtype=jnp.int32)[:, None]
    inv_freq = ROPE_THETA ** (-jnp.arange(0, hd, 2, dtype=F32) / hd)
    angles = pos.astype(F32) * jnp.concatenate([inv_freq, inv_freq])[None, :]
    return jnp.cos(angles), jnp.sin(angles)


def solution(mesh):
    groups = mesh.shape["cp"]
    tps = mesh.shape["tp"]

    def local_layer(x_loc, kp_loc, vp_loc, norm_attn, w_query, w_key, w_value, w_out, norm_mlp, w_gate, w_up, w_down):
        rows = x_loc.shape[0]
        pre_dev, kv_loc, hd = kp_loc.shape
        flat = (pre_dev, kv_loc * hd)
        tables = angle_tables(lax.axis_index("cp"), groups, rows // 2, pre_dev * groups, hd)

        def attention(exact):
            return attention_call(
                exact, x_loc, kp_loc.reshape(flat), vp_loc.reshape(flat), *tables, norm_attn, w_query, w_key, w_value, w_out, groups, tps
            )

        k_new, v_new, o_early, o_late, w_out_all, plain = attention(False)
        o_early, o_late = lax.cond(plain[0, 0] == 1, lambda: (o_early, o_late), lambda: tuple(attention(True)[2:4]))
        x_out = mlp_call(x_loc, o_early, o_late, w_out, w_out_all, norm_mlp, w_gate, w_up, w_down, tps)[0]
        return x_out, k_new.reshape(rows, kv_loc, hd), v_new.reshape(rows, kv_loc, hd)

    row_spec = P(("dp", "cp"), None)
    kv_spec = P(("dp", "cp"), "tp", None)
    col_spec = P(None, "tp")
    row_split = P("tp", None)
    vec_spec = P(None)
    return jax.shard_map(
        local_layer,
        mesh=mesh,
        in_specs=(row_spec, kv_spec, kv_spec, vec_spec, col_spec, col_spec, col_spec, row_split, vec_spec, col_spec, col_spec, row_split),
        out_specs=(row_spec, kv_spec, kv_spec),
        check_vma=False,
    )
```

time: 1260 us -> 326 us (0.26)
  waiting for transfers between devices: 516 us -> 0 us
  matrix products: 434 us -> 0 us
  Pallas kernels: 0 us -> 312 us
  other arithmetic: 240 us -> 1.04 us
  local copies, waits for them, and re-layouts: 35.4 us -> 11.1 us
  starting transfers between devices: 18.2 us -> 0 us
  between operations: 14.6 us -> 1.32 us
    psum x2 -> x0, waiting for transfers between devices: 450 us -> none  [the longest x1 231 us: local_layer(): lax.psum(jnp.dot(attn_heads, w_out, preferred_element_type=jnp.float32),...]
    dot_general x23 -> x0, matrix products: 434 us -> none  [the longest x8 190 us: attend_step(): jnp.einsum('sgrk,kgd->sgrd', weights.astype(jnp.bfloat16), v_blk, preferr...]
    pallas_call x0 -> x2, Pallas kernels: none -> 312 us  [the longest x1 185 us: mlp_call(): pl.pallas_call(kernel, in_specs=[HBM] * 5 + [VMEM] + [HBM] * 3, out_specs...]
    reduce_sum x10 -> x0, other arithmetic: 189 us -> none  [the longest x8 176 us: attend_step(): denom_sum = denom_sum * correction + jnp.sum(weights, axis=-1)]
    ppermute x14 -> x0, waiting for transfers between devices: 65.5 us -> none  [step_body(): k_cur, v_cur = lax.ppermute((k_cur, v_cur), 'cp', perm_pairs)]
    convert_element_type x5 -> x0, other arithmetic: 25.4 us -> none  [the longest x1 14.5 us: local_layer(): (resid_mid + lax.psum(jnp.dot(act_mid, w_down, preferred_element_type=jnp...]
    le x8 -> x0, other arithmetic: 18.5 us -> none  [attend_step(): visible = (k_pos[None, :] <= q_pos[:, None])[:, None, None, :]]
    ppermute x14 -> x0, starting transfers between devices: 18.1 us -> none  [step_body(): k_cur, v_cur = lax.ppermute((k_cur, v_cur), 'cp', perm_pairs)]
  transfers between devices with their start and end apart: 16 -> 0, of which waited for: 9 -> 0; matrix products, arithmetic and copies ran while one was open for 26% -> 0% of each run, Pallas kernels for 0% -> 0%
where the time goes in v1:
time: 326 us; the launch traced here: 325 us
  Pallas kernels  312 us (96%)
  local copies, waits for them, and re-layouts  11.1 us (3%)
    pallas_call x1, Pallas kernels, mlp_call(): pl.pallas_call(kernel, in_specs=[HBM] * 5 + [VMEM] + [HBM] * 3, out_specs...  185 us
    pallas_call x1, Pallas kernels, attention_call(): pl.pallas_call(kernel, in_specs=[HBM] * 3 + [VMEM] * 3 + [HBM] * 4, out_s...  126 us

profile of v1, /device:TPU:97, one launch (start us, length us, event | category | flops | bytes accessed | tf_op | source)
XLA Modules:
  0.0 325.4 jit_solution(4442518331512256653)
XLA Ops:
  0.7 0.1 pad_maximum_fusion
  0.7 0.9 fusion
  1.7 2.3 copy_bitcast_fusion.2
  4.0 0.0 copy-start.1
  4.0 126.2 %attention.1 = (bf16[1024,256]{1,0:T(8,128)(2,1)}, bf16[1024,256]{1,0:T(8,128)(2,1)}, bf16[512,3072]{1,0:T(8,128)(2,1)}, bf16[512,3072]{1,0:T(8,128)(2,1)}, bf16[3072,3072]{1,0:T(8,128)(2,1)}, /*index=5*/s32[1,1]{1,0:T(1,128)}) custom-call(bf16[1024,3072]{1,0:T(8,128)(2,1)} %x_hbm.3, bf16[1024,256]{1,0:T(8,128)(2,1)} %get-tuple-element.62.kp_hbm, ...), custom_call_target="tpu_custom_call" | custom-call | tf_op jit(solution)/shard_map/attention/pallas_call | solution.py:650
  130.9 0.0 copy-done.1
  130.9 0.3 conditional.1
  131.2 0.0 copy-start
  131.2 185.4 %mlp.1 = (bf16[1024,3072]{1,0:T(8,128)(2,1)}, bf16[512,3072]{1,0:T(8,128)(2,1)}) custom-call(bf16[1024,3072]{1,0:T(8,128)(2,1)} %x_hbm.3, bf16[512,3072]{1,0:T(8,128)(2,1)} %get-tuple-element.51.oe_hbm, bf16[512,3072]{1,0:T(8,128)(2,1)} %get-tuple-element.52.ol_in, bf16[768,3072]{1,0:T(8,128)(2,1)} %wo_hbm.3, ...), custom_call_target="tpu_custom_call", output_to_operand_aliasing={{1}: (2, {})} | custom-call | tf_op jit(solution)/shard_map/mlp/pallas_call | solution.py:866
  316.6 2.0 reshape.40
  318.5 0.0 copy-done
  318.5 0.9 reshape.41
  319.4 5.9 %copy.30 = bf16[1024,3072]{1,0:T(8,128)(2,1)} copy(bf16[1024,3072]{1,0:T(8,128)(2,1)} %get-tuple-element.70) | data formatting | bytes 12582912
  (2 shorter events, 0.0 us)
Async XLA Ops:
  4.0 126.9 %copy-start.1 = (bf16[3072]{0:T(1024)(128)(2,1)S(1)}, bf16[3072]{0:T(1024)(128)(2,1)}, u32[]{:S(2)}) copy-start(bf16[3072]{0:T(1024)(128)(2,1)} %g_ref.2) | copy-start | bytes 18436
  131.2 187.3 %copy-start = (bf16[1024,256]{1,0:T(8,128)(2,1)S(1)}, bf16[1024,256]{1,0:T(8,128)(2,1)}, u32[]{:S(2)}) copy-start(bf16[1024,256]{1,0:T(8,128)(2,1)} %get-tuple-element.56) | copy-start | bytes 1572868

commit v2 on v1

v2 whole, which is shorter than its diff:
```python
import jax
import jax.numpy as jnp
from jax import lax
from jax.experimental import pallas as pl
from jax.experimental.pallas import tpu as pltpu
from jax.sharding import PartitionSpec as P

ROPE_THETA = 500000.0
NORM_EPS = 1e-5
LOG2E = 1.4426950408889634
F32 = jnp.float32
BF16 = jnp.bfloat16
MESH = pl.DeviceIdType.MESH
LANES = 128
SUB = 8
TILE = 256
NORM_ROWS = 32
WIDE = 512
VMEM_LIMIT = 67043328
S_LIMIT, V_LIMIT = 60.0, 40.0
HBM = pl.BlockSpec(memory_space=pl.ANY)
VMEM = pl.BlockSpec(memory_space=pltpu.VMEM)
(KP, VP, KE, VE, KL, VL, QE, QL, OE, OL) = range(10)
(K_RIGHT, V_RIGHT, K_LEFT, V_LEFT, K_ON, V_ON) = range(6)
(P_OWN, P_SIB, EARLY, LATE) = range(4)
(UP, DOWN, ON_UP, ON_DOWN) = range(4)
(FAR_R, FAR_L, NEAR_R, NEAR_L, SUM_R, SUM_L, OUT_R, OUT_L, ON_R, ON_L) = range(10)


def scoped(name):
    def deco(f):
        def g(*a):
            with jax.named_scope(name):
                return f(*a)

        return g

    return deco


def dma(*shape):
    return pltpu.SemaphoreType.DMA(shape)


def start(copies):
    for c in copies:
        c.start()


def span(at, size, unit=LANES):
    return pl.ds(pl.multiple_of(at, unit), size)


def both(v):
    return lax.rem(v, 2)


def fold_rows(values, op):
    rows, cols = values.shape
    return op(values.reshape(rows // SUB, SUB, cols), axis=0)


def rms(x):
    return x * lax.rsqrt(jnp.mean(x * x, axis=-1, keepdims=True) + NORM_EPS)


def loop(n, body):
    lax.fori_loop(0, n, lambda i, c: (body(i), c)[1], 0)


def remote(src, dst, sems, i, who):
    send, recv = sems
    return pltpu.make_async_remote_copy(src_ref=src, dst_ref=dst, send_sem=send.at[i], recv_sem=recv.at[i], device_id=who, device_id_type=MESH)


def gather_steps(at, sems, ranks, src=None):
    here, up, down, over, size = ranks
    half = size // 2
    to_up, to_down = {"tp": up}, {"tp": down}

    def move(i, rank, first, n, who, other=None):
        ref = at(rank, first, n)
        return remote(ref if other is None else other, ref, sems, i, who)

    sends = [
        move(UP, here, 0, size, to_up, src),
        move(DOWN, here, 0, size, to_down, src),
        move(ON_UP, down, 0, half, to_up),
        move(ON_DOWN, up, half, half, to_down),
    ]
    brings = [
        move(UP, down, 0, size, to_up),
        move(DOWN, up, 0, size, to_down),
        move(ON_UP, over, 0, half, to_up),
        move(ON_DOWN, over, half, half, to_down),
    ]
    return sends, brings


def layer_call(exact, x_loc, kp2, vp2, cos_tab, sin_tab, norm_attn, w_query, w_key, w_value, w_out, norm_mlp, w_gate, w_up, w_down, groups, tps):
    rows, d = x_loc.shape
    blk = rows // 2
    hd = kp2.shape[2]
    heads = w_query.shape[1] // hd
    ratio = heads // 2
    pre = kp2.shape[0]
    chips = groups // 2
    assert chips == tps == 4 and pre == rows and hd == LANES and ratio == 3
    deep = 2 * blk
    n_wide = heads * hd
    side = ratio * 2 * blk
    half_side = side // 2
    per_chip = 2 * pre
    suf = chips * per_chip
    send = suf + chips * 2 * rows
    send_pre = send + rows
    d_out = w_out.shape[1]
    w_half = (d_out - WIDE) // 2
    w_rows = w_out.shape[0]
    w_part = w_rows // groups
    scale = LOG2E * hd**-0.5
    n_proj = n_wide + 4 * hd
    d_in = tps * n_wide
    ff = w_gate.shape[1]
    n_chunks = rows // TILE
    quarter = TILE // tps
    half = quarter // 2
    gate = WIDE // 2
    n_a, n_b, n_c = d // WIDE, ff // gate, d // WIDE
    per = n_a + n_b + n_c
    total = per * n_chunks
    slots = 3

    def kernel(x_hbm, kp_hbm, vp_hbm, cos_ref, sin_ref, g_ref, wq_hbm, wk_hbm, wv_hbm, wo_hbm, g2_ref, wg_hbm, wu_hbm, wd_hbm,
               k_out, v_out, out_hbm, o_hbm, wall_hbm, wlast_hbm, plain_out,
               w_buf, x_buf, h_0, h_1, q3, keys, vals, kp_buf, vp_buf, l_ref, a_ref, o_st, o_snd, size_all, size_tp,
               o_buf, act_buf, part, got1, got2, y_own, fin, *rest):
        if exact:
            m_ref, *rest = rest
        l_sem, x_sem, sw_s, sw_r, x_s, x_r, w_s, w_r, d_s, d_r, o_s, o_r, z_s, z_r, y_s, y_r, e_s, e_r, t_sem, c_s, c_r, c_sem = rest
        me, t = lax.axis_index("cp"), lax.axis_index("tp")
        core, chip = both(me), lax.div(me, 2)
        sib = {"cp": me + 1 - 2 * core}
        x_right, x_left = {"cp": lax.rem(me + 2, groups)}, {"cp": lax.rem(me + groups - 2, groups)}
        up, down, over = [lax.rem(t + j, tps) for j in (1, tps - 1, 2)]

        def local(i, src, dst):
            return pltpu.make_async_copy(src, dst, l_sem.at[i])

        def x_copy(i):
            return pltpu.make_async_copy(x_hbm.at[span(i * TILE, TILE)], x_buf.at[both(i)], x_sem.at[both(i)])

        vp_copy = local(0, vp_hbm, vp_buf)
        kp_copy = local(1, kp_hbm, kp_buf)
        pair_w = 2 * hd

        def proj_w(pair):
            return pair * pair_w // WIDE, pl.ds(pair * pair_w % WIDE, pair_w)

        w_copies = []
        for pair in range(n_proj // pair_w):
            src, first = (wq_hbm, pair) if pair < ratio else ((wk_hbm, wv_hbm)[pair - ratio], 0)
            slot, lanes = proj_w(pair)
            w_copies.append(local(2 + pair, src.at[:, pl.ds(first * pair_w, pair_w)], w_buf.at[slot, :, lanes]))
        start([vp_copy, kp_copy, x_copy(0)] + w_copies + [x_copy(1)])

        greeted = [{"cp": lax.rem(me + j, groups)} for j in range(1, groups)] + [{"tp": lax.rem(t + j, tps)} for j in range(1, tps)]
        barrier = pltpu.get_barrier_semaphore()
        for who in greeted:
            pl.semaphore_signal(barrier, inc=1, device_id=who, device_id_type=MESH)

        def w_place(which):
            return lambda rank, first, size: wall_hbm.at[span(rank * w_rows + first, size), span(which * w_half, w_half)]

        w_ranks = (t, up, down, over, w_rows)
        w_sends, w_brings = gather_steps(w_place(core), (w_s, w_r), w_ranks, wo_hbm.at[:, span(core * w_half, w_half)])
        w_theirs = gather_steps(w_place(1 - core), (d_s, d_r), w_ranks)[1]

        def part_rows(who):
            return span(who * w_part, w_part, SUB)

        y_steps, x_steps, d_steps = range(tps - 1), range(tps - 1, 2 * (tps - 1)), range(2 * (tps - 1), 3 * tps - 2)

        def w_last(i, arriving=False):
            if i in y_steps:
                src = wo_hbm.at[part_rows(me), pl.ds(2 * w_half, WIDE)]
                return remote(src, wlast_hbm.at[y_steps[-1] - i, part_rows(me)], (e_s, e_r), i, {"tp": lax.rem(t + i + 1, tps)})
            back = 2 * (i - d_steps[0])
            if i in x_steps:
                back = 2 * (i - y_steps[-1])
                to = {"cp": lax.rem(me + back, groups)}
                owner = lax.rem(me + groups - back, groups) if arriving else me
            else:
                to, owner = sib, lax.rem(me + groups - back, groups)
                if arriving:
                    owner = owner + 1 - 2 * core
            ref = wlast_hbm.at[:, part_rows(owner)]
            return remote(ref, ref, (e_s, e_r), i, to)

        def w_last_round():
            for i in y_steps:
                w_last(i, True).wait_recv()
            start([w_last(i) for i in x_steps] + [w_last(d_steps[0])])

        @scoped("w_last_on")
        def w_last_on():
            for i in x_steps:
                w_last(i, True).wait_recv()
            start([w_last(i) for i in d_steps[1:]])

        @scoped("w_last_here")
        def w_last_here():
            for i in d_steps:
                w_last(i, True).wait_recv()

        def w_share(i):
            ref = w_brings[i].dst_ref
            return remote(ref, ref, (d_s, d_r), i, sib)

        def o_cols(which):
            return span(which * ratio * hd, ratio * hd)

        def swap(i, arriving=False):
            if i == KP:
                src, dst = keys.at[pl.ds(send_pre, pre)], keys.at[pl.ds(pre, pre)]
            elif i == VP:
                src, dst = vals.at[pl.ds(send_pre, pre)], vals.at[pl.ds(pre, pre)]
            elif i in (KE, VE, KL, VL):
                buf, late = keys if i in (KE, KL) else vals, i in (KL, VL)
                src, dst = buf.at[pl.ds(send + late * blk, blk)], buf.at[pl.ds(suf + late * deep + blk, blk)]
            elif i in (QE, QL):
                at = pl.ds((i - QE) * half_side, half_side)
                src, dst = q3.at[2, :, at], q3.at[1, :, at]
            else:
                src, dst = o_snd.at[i - OE], o_st.at[i - OE, :, o_cols(1 - core if arriving else core)]
            return remote(src, dst, (sw_s, sw_r), i, sib)

        def region(item, slot):
            if item in (P_OWN, P_SIB):
                return pl.ds(slot * per_chip + item * pre, pre)
            return pl.ds(suf + (2 * slot + item - EARLY) * deep, deep)

        def ring(item):
            plan = {K_RIGHT: (keys, 0, 1, x_right), V_RIGHT: (vals, 0, 1, x_right), K_LEFT: (keys, 0, 3, x_left), V_LEFT: (vals, 0, 3, x_left),
                    K_ON: (keys, 1, 2, x_right), V_ON: (vals, 3, 2, x_left)}
            return [remote(buf.at[region(item, a)], buf.at[region(item, b)], (x_s.at[item], x_r.at[item]), i, who) for i, (buf, a, b, who) in plan.items()]

        @scoped("ring_on")
        def pass_on(item):
            got = ring(item)
            got[K_RIGHT].wait_recv()
            got[K_ON].start()
            got[V_LEFT].wait_recv()
            got[V_ON].start()

        @scoped("wait_sides")
        def sides_here(item):
            got = ring(item)
            got[V_RIGHT].wait_recv()
            got[K_LEFT].wait_recv()

        @scoped("wait_far")
        def far_here(item):
            got = ring(item)
            got[K_ON].wait_recv()
            got[V_ON].wait_recv()

        h_bufs = (h_0, h_1)

        def norm(i, slot):
            g = g_ref[...].astype(F32)[None, :]
            for r in range(0, TILE, NORM_ROWS):
                h_bufs[slot][r : r + NORM_ROWS, :] = (rms(x_buf[slot, r : r + NORM_ROWS, :].astype(F32)) * g).astype(BF16)

        def project(i, slot):
            h_tile = h_bufs[slot]
            late, sub = lax.div(i, blk // TILE), lax.rem(i, blk // TILE)
            at_rows = span(i * TILE, TILE)
            tab = span(sub * TILE, TILE)
            first = lax.broadcasted_iota(jnp.int32, (TILE, hd), 1) < hd // 2

            def table(ref):
                v = ref[tab, :]
                w = pltpu.roll(v, hd // 2, 1)
                return jnp.where(first == (late == 0), v, w)

            cos, sin = table(cos_ref), table(sin_ref)
            sin = jnp.where(first, -sin, sin)

            def rope(v):
                return v * cos + pltpu.roll(v, hd // 2, 1) * sin

            for pair in range(n_proj // pair_w):
                slot, w_lanes = proj_w(pair)
                out = jnp.dot(h_tile[...], w_buf[slot, :, w_lanes], preferred_element_type=F32)
                heads_new = []
                for hh in range(2):
                    v = out[:, hh * hd : (hh + 1) * hd]
                    head = 2 * pair + hh
                    at = jnp.where(core == hh, suf + late * deep, send + late * blk) + sub * TILE
                    if head < heads:
                        q_t = rope(v).astype(BF16).astype(F32).T
                        if not exact:
                            n2 = jnp.max(jnp.sum(fold_rows(q_t * q_t, jnp.sum), axis=0, keepdims=True), axis=1, keepdims=True)
                            note(0, jnp.broadcast_to(n2, (1, LANES)))
                        q_t = q_t * scale
                        hi = q_t.astype(BF16)
                        idx = jnp.where(core == head // ratio, 0, 2)
                        col = span(late * half_side + (head % ratio) * blk + sub * TILE, TILE)
                        q3[idx, pl.ds(0, hd), col] = hi
                        q3[idx, pl.ds(hd, hd), col] = (q_t - hi.astype(F32)).astype(BF16)
                    elif head < heads + 2:
                        k = rope(v).astype(BF16)
                        keys[span(at, TILE), :] = k
                        heads_new.append(k)
                        note_rows(1, k.astype(F32))
                    else:
                        v = v.astype(BF16)
                        heads_new.append(v)
                        v_t = v.astype(F32).T
                        note_size(2, v.astype(F32))
                        for b in range(0, TILE, LANES):
                            vals[span(at + b, LANES), :] = v_t[:, b : b + LANES].astype(BF16)
                if heads_new:
                    (kp_buf, vp_buf)[pair - ratio][at_rows] = jnp.concatenate(heads_new, axis=1).reshape(TILE, 2, hd)

        kp_copy.wait()
        vp_copy.wait()
        if not exact:
            size_all[0] = jnp.zeros(size_all.shape[1:], F32)

        def note(i, v):
            if not exact:
                size_all[0, i : i + 1, :] = jnp.maximum(size_all[0, i : i + 1, :], v)

        def note_rows(i, v):
            if not exact:
                n2 = jnp.sum(v * v, axis=1, keepdims=True)
                note(i, jnp.broadcast_to(jnp.max(n2, axis=0, keepdims=True), (1, LANES)))

        def note_size(i, v):
            if not exact:
                note(i, jnp.max(fold_rows(jnp.abs(v), jnp.max), axis=0, keepdims=True))

        def split_prefix(b):
            rows_b = span(b * LANES, LANES)
            k, v = [buf[rows_b].reshape(LANES, 2 * hd) for buf in (kp_buf, vp_buf)]
            for j in range(2):
                at = span(jnp.where(core == j, 0, send_pre) + b * LANES, LANES)
                k_j, v_j = k[:, j * hd : (j + 1) * hd], v[:, j * hd : (j + 1) * hd].astype(F32)
                keys[at, :] = k_j
                vals[at, :] = v_j.T.astype(BF16)
                note_rows(1, k_j.astype(F32))
                note_size(2, v_j)

        loop(pre // LANES, split_prefix)
        x_copy(0).wait()
        norm(0, 0)
        pl.semaphore_wait(barrier, len(greeted))
        start([swap(KP), swap(VP)] + ring(P_OWN)[:K_ON] + [w_last(i) for i in y_steps] + w_sends[:ON_UP])
        with jax.named_scope("w_wait"):
            for c in w_copies:
                c.wait()

        n_tiles = rows // TILE

        @scoped("project")
        def two_tiles(j):
            i = 2 * j
            x_copy(i + 1).wait()

            @pl.when(i + 2 < n_tiles)
            def _():
                x_copy(i + 2).start()

            norm(i + 1, 1)
            project(i, 0)

            @pl.when(j == 0)
            def _():
                swap(KP).wait_recv()
                swap(VP).wait_recv()
                start(ring(P_SIB)[:K_ON])

            @pl.when(i + 2 < n_tiles)
            def _():
                x_copy(i + 3).start()
                x_copy(i + 2).wait()

            norm(i + 2, 0)
            project(i + 1, 1)

            @pl.when(j == 0)
            def _():
                start([swap(i) for i in (KE, VE, QE)])

        loop(n_tiles // 2, two_tiles)
        start([swap(i) for i in (KL, VL, QL)])
        new_copies = [local(4, kp_buf, k_out), local(5, vp_buf, v_out)]
        start(new_copies)

        def size_copies():
            out = []
            for j in range(1, groups):
                out.append(remote(size_all.at[0], size_all.at[j], (z_s, z_r), j, {"cp": lax.rem(me + j, groups)}))
            return out

        def size_on():
            return [remote(size_tp.at[0], size_tp.at[j], (y_s, y_r), j, {"tp": lax.rem(t + j, tps)}) for j in range(1, tps)]

        def sizes_meet():
            for c in size_copies():
                c.wait_recv()
            size_tp[0] = jnp.max(size_all[...], axis=0)
            start(size_on())

        if not exact:
            start(size_copies())
        if exact:
            m_ref[...] = jnp.full_like(m_ref, -jnp.inf)
        l_ref[...] = jnp.zeros_like(l_ref)
        a_ref[...] = jnp.zeros_like(a_ref)
        with jax.named_scope("swap_wait"):
            for i in range(KE, OE):
                swap(i).wait_recv()

        p_bufs = (o_buf, act_buf)

        def beside(r):
            return pl.ds(r // TILE * blk, blk)

        lead = 0 if exact else 1
        main_unroll = 1 if exact else 4

        def state_at(step):
            who, late, head = step[:3]
            return span(who * side + late * half_side + head * blk, blk)

        def product(step, r, n, shifts):
            who, late, head, key = step
            k = keys[span(key + r, n), :]
            s = jnp.dot(jnp.concatenate([k, k], axis=1), q3[who, :, span(late * half_side + head * blk, blk)], preferred_element_type=F32)
            if shifts is not None:
                row = lax.broadcasted_iota(jnp.int32, s.shape, 0) + r % blk
                col = lax.broadcasted_iota(jnp.int32, s.shape, 1) + shifts[r // blk]
                s = jnp.where(row <= col, s, -jnp.inf)
            return s

        def weights(step, slot, shifts):
            total = None
            for r in range(0, deep, TILE):
                p = jnp.exp2(product(step, r, TILE, shifts))
                p_bufs[slot][:, beside(r)] = p.astype(BF16)
                t8 = fold_rows(p, jnp.sum)
                total = t8 if total is None else total + t8
            l_ref[:, state_at(step)] += total

        def values(step, slot):
            v = jnp.concatenate([vals[span(step[3] + b, LANES), :] for b in range(0, deep, LANES)], axis=1)
            p = jnp.concatenate([p_bufs[slot][:, beside(r)] for r in range(0, deep, TILE)], axis=0)
            a_ref[:, state_at(step)] += jnp.dot(v, p, preferred_element_type=F32)

        def exact_step(step, shifts):
            cols = state_at(step)
            top = m_old = m_ref[:, cols]
            for r in range(0, deep, TILE):
                s = product(step, r, TILE, shifts)
                part[0, :, beside(r)] = s
                top = jnp.maximum(top, jnp.max(s, axis=0, keepdims=True))
            corr = jnp.exp2(m_old - top)
            m_ref[:, cols] = top
            total = l_ref[:, cols] * corr
            for r in range(0, deep, TILE):
                p = jnp.exp2(part[0, :, beside(r)] - top)
                o_buf[:, beside(r)] = p.astype(BF16)
                total += fold_rows(p, jnp.sum)
            l_ref[:, cols] = total
            a_ref[:, cols] = a_ref[:, cols] * corr
            values(step, 0)

        def run(n_steps, unroll, where, service, mask=None):
            def shifts(step):
                return None if mask is None else mask(step)

            def ahead(u, slot):
                weights(where(u), slot, shifts(where(u)))

            if not exact:
                ahead(0, 0)

            @scoped("body")
            def body(i):
                service(i)
                for j in range(unroll):
                    u = unroll * i + j
                    if exact:
                        exact_step(where(u), shifts(where(u)))
                    else:
                        ahead(u + 1, (j + 1) % 2)
                        values(where(u), j % 2)

            trips = (n_steps - lead) // unroll
            loop(trips, body)
            for u in range(unroll * trips, n_steps):
                if u + 1 < n_steps:
                    ahead(u + 1, (u + 1) % 2)
                values(where(u), u % 2)

        def own_where(u):
            who, rest = lax.div(u, 2 * ratio), lax.rem(u, 2 * ratio)
            late, head = lax.div(rest, ratio), lax.rem(rest, ratio)
            return who, late, head, suf + late * deep

        def own_mask(step):
            who, late = step[:2]
            q_core = jnp.where(who == 0, core, 1 - core)
            seen = jnp.where(late == 0, q_core, 1 - q_core)
            other = (2 * seen - 1) * blk
            return jnp.where(who == 0, 0, other), jnp.where(who == 0, other, 0)

        with jax.named_scope("run_own"):
            run(4 * ratio, 1 if exact else 2, own_where, lambda i: None, own_mask)

        qt = 2 * ratio
        pc = per_chip // deep
        n_rem = chips - 1
        n_near = jnp.minimum(chip, 1) + lax.div(chip, n_rem)
        b1 = 2 * qt * pc
        b2 = b1 + qt
        b4 = b2 + n_rem * qt * pc
        b5 = b4 + qt * n_near
        b6 = b5 + qt * pc
        b7 = b6 + qt * (chip - n_near)
        b8 = b7 + (n_rem - 1) * qt * pc
        b9 = b8 + qt * n_rem
        n_main = b4 + n_rem * qt * pc + 2 * qt * n_rem

        def where(u):
            def prefix(j, skip=0):
                i, r = lax.div(j, qt * pc) + skip, lax.rem(j, qt * pc)
                return lax.div(r, pc), far_last(i) * per_chip + lax.rem(r, pc) * deep

            def far_last(i):
                return jnp.where(i == 0, 1, jnp.where(i == 1, n_rem, 2))

            def suffix(j, back):
                return lax.rem(j, qt), suf + back * 2 * deep

            tile = lax.div(u, pc)
            late = lax.div(tile, qt)
            q_i, key = lax.rem(tile, qt), lax.rem(u, pc) * deep
            j9 = suffix(u - b9, far_last(jnp.minimum(chip, 1) + lax.div(u - b9, qt)))
            for first, is_late, (q_n, key_n) in (
                (b1, 1, (u - b1, suf)),
                (b2, 0, prefix(u - b2)),
                (b4, 0, suffix(u - b4, far_last(lax.div(u - b4, qt)))),
                (b5, 1, prefix(u - b5)),
                (b6, 0, suffix(u - b6, 2)),
                (b7, 1, prefix(u - b7, 1)),
                (b8, 1, (lax.div(u - b8, n_rem), suf + (1 + lax.rem(u - b8, n_rem)) * 2 * deep)),
                (b9, 1, (j9[0], j9[1] + deep)),
            ):
                here = u >= first
                late, q_i, key = [jnp.where(here, a, b) for a, b in ((is_late, late), (q_n, q_i), (key_n, key))]
            return lax.div(q_i, ratio), late, lax.rem(q_i, ratio), key

        @scoped("finalize")
        def finalize(h):
            def one(u):
                who, head = lax.div(u, ratio), lax.rem(u, ratio)
                at = state_at((who, h, head))
                inv = 1.0 / jnp.sum(l_ref[:, at], axis=0, keepdims=True)
                o = (a_ref[:, at] * inv).T.astype(BF16)

                @pl.when(who == 0)
                def _():
                    o_st[h, :, span(core * ratio * hd + head * hd, hd)] = o

                @pl.when(who == 1)
                def _():
                    o_snd[h, :, span(head * hd, hd)] = o

            loop(2 * ratio, one)
            swap(OE + h).start()

        gathers, o_keeps = [], []
        for i, (h, first, n) in enumerate(((0, 0, TILE), (0, TILE, blk - TILE), (1, 0, blk))):
            place = lambda rank, at, size, base=h * blk + first: o_hbm.at[pl.ds(base + at, size), span(rank * n_wide, n_wide)]
            src = o_st.at[h, pl.ds(first, n)]
            gathers.append(gather_steps(place, (o_s.at[i], o_r.at[i]), (t, up, down, over, n), src))
            o_keeps.append(local(i, src, place(t, 0, n)))

        def gather_on(i):
            sends, brings = gathers[i]
            for b, s in zip(brings, sends[ON_UP:]):
                b.wait_recv()
                s.start()

        def gathered(i):
            for b in gathers[i][1][ON_UP:]:
                b.wait_recv()
            o_keeps[i].wait()

        def tile_copies(kind, i, slot):
            def get(j, src, dst):
                return pltpu.make_async_copy(src, dst, t_sem.at[slot, j])

            if kind in (0, 3):
                cols, out = span(i * WIDE, WIDE), []
                for j in range(tps):
                    rank = lax.rem(t + j, tps)
                    at = span(rank * n_wide, n_wide)
                    src = wo_hbm.at[:, cols] if j == 0 else wlast_hbm.at[j - 1] if kind == 3 else wall_hbm.at[at, cols]
                    out.append(get(j, src, w_buf.at[slot, at]))
                return out
            if kind == 1:
                at = span(i * gate, gate)
                return [get(j, w.at[:, at], w_buf.at[slot, :, pl.ds(j * gate, gate)]) for j, w in enumerate((wg_hbm, wu_hbm))]
            return [get(0, wd_hbm.at[:, span(i * WIDE, WIDE)], w_buf.at[slot, pl.ds(0, ff)])]

        def fetch(g):
            i, slot = lax.rem(g, per), lax.rem(g, slots)
            last_a = n_a - 1
            pl.when(g == 3)(w_last_on)
            pl.when(g == last_a)(w_last_here)
            for kind, first, n in ((0, 0, last_a), (3, last_a, 1), (1, n_a, n_b), (2, n_a + n_b, n_c)):
                pl.when((g < total) & (i >= first) & (i < first + n))(lambda: start(tile_copies(kind, last_a if kind == 3 else i - first, slot)))

        def mlp_x(c):
            return pltpu.make_async_copy(x_hbm.at[span(c * TILE, TILE)], x_buf.at[both(c)], x_sem.at[both(c)])

        def start_x(c):
            mlp_x(c).start()

        def o_rows(c):
            return local(3, o_hbm.at[span(c * TILE, TILE)], o_buf)

        def out_rows(c, q, first, n):
            return out_hbm.at[span(c * TILE + q * quarter + first, n, half)]

        def at_rows(q, first, n):
            return span(q * quarter + first, n, half)

        def moves(c):
            def go(i, src, dst):
                return remote(src, dst, (c_s.at[c], c_r.at[c]), i, {"tp": up if i % 2 == 0 else down})

            def mine(q, first):
                return part.at[both(c), at_rows(q, first, half)]

            top, low = pl.ds(0, half), pl.ds(half, half)
            sends = {
                FAR_R: (mine(over, 0), got1.at[c, 0]),
                FAR_L: (mine(over, half), got1.at[c, 1]),
                NEAR_R: (mine(up, half), got2.at[c, 0, low]),
                NEAR_L: (mine(down, 0), got2.at[c, 1, top]),
                SUM_R: (mine(up, 0), got2.at[c, 0, top]),
                SUM_L: (mine(down, half), got2.at[c, 1, low]),
                OUT_R: (fin.at[c], out_rows(c, t, 0, quarter)),
                OUT_L: (fin.at[c], out_rows(c, t, 0, quarter)),
                ON_R: (out_rows(c, down, 0, half), out_rows(c, down, 0, half)),
                ON_L: (out_rows(c, up, half, half), out_rows(c, up, half, half)),
            }
            brings = {
                OUT_R: (fin.at[c], out_rows(c, down, 0, quarter)),
                OUT_L: (fin.at[c], out_rows(c, up, 0, quarter)),
                ON_R: (out_rows(c, over, 0, half), out_rows(c, over, 0, half)),
                ON_L: (out_rows(c, over, half, half), out_rows(c, over, half, half)),
            }
            return [go(i, *s) for i, s in sends.items()], {i: go(i, *s) for i, s in brings.items()}

        def own_copy(c):
            return pltpu.make_async_copy(fin.at[c], out_rows(c, t, 0, quarter), c_sem.at[c])

        @scoped("middle")
        def middle(c):
            m = moves(c)[0]
            for way, q, first in ((0, up, 0), (1, down, half)):
                m[FAR_R + way].wait_recv()
                part[both(c), at_rows(q, first, half), :] += got1[c, way]
                m[SUM_R + way].start()

        @scoped("finish")
        def finish(c):
            m = moves(c)[0]
            for i in (NEAR_R, NEAR_L, SUM_R, SUM_L):
                m[i].wait_recv()
            fin[c] = (y_own[both(c)] + (part[both(c), at_rows(t, 0, quarter), :] + (got2[c, 0] + got2[c, 1]))).astype(BF16)
            own_copy(c).start()
            start(m[OUT_R:ON_R])

        @scoped("forward")
        def forward(c):
            m, b = moves(c)
            for way in range(2):
                b[OUT_R + way].wait_recv()
                m[ON_R + way].start()

        @scoped("drain")
        def drain(c):
            m, b = moves(c)
            b[ON_R].wait_recv()
            b[ON_L].wait_recv()
            for s in m[OUT_R:]:
                s.wait_send()
            own_copy(c).wait()

        def release(c):
            for s in moves(c)[0][:OUT_R]:
                s.wait_send()

        def tiles(n, base, kind, body):
            @scoped("tile_" + "abc"[kind])
            def one(i):
                g = base + i
                fetch(g + 2)
                slot = lax.rem(g, slots)
                at = jnp.minimum(i, n_a - 2) if kind == 0 else i
                for cp in tile_copies(kind, at, slot):
                    cp.wait()
                body(i, slot)

            loop(n, one)

        def chunk_step(c):
            base, slot_c = c * per, both(c)
            for i in range(3):
                pl.when(c == i)(lambda i=i: gathered(i))
            o_rows(c).start()
            pl.when(c >= 2)(lambda: release(c - 2))
            mlp_x(c).wait()
            pl.when(c + 1 < n_chunks)(lambda: start_x(c + 1))
            o_rows(c).wait()

            def tile_a(i, slot):
                at = span(i * WIDE, WIDE)
                part[slot_c, :, at] = x_buf[slot_c, :, at].astype(F32) + jnp.dot(o_buf[...], w_buf[slot], preferred_element_type=F32)

            tiles(n_a, base, 0, tile_a)
            y_own[both(c)] = part[slot_c, span(t * quarter, quarter, quarter), :]

            def norm2(i):
                at = span(i * NORM_ROWS, NORM_ROWS, NORM_ROWS)
                h_0[at, :] = (rms(part[slot_c, at, :]) * g2_ref[...].astype(F32)[None, :]).astype(BF16)

            loop(TILE // NORM_ROWS, norm2)
            pl.when(c == 0)(lambda: gather_on(1))
            pl.when(c >= 1)(lambda: middle(c - 1))

            def tile_b(i, slot):
                pair = jnp.dot(h_0[...], w_buf[slot], preferred_element_type=F32)
                act_buf[:, span(i * gate, gate)] = (jax.nn.silu(pair[:, :gate]) * pair[:, gate:]).astype(BF16)

            tiles(n_b, base + n_a, 1, tile_b)
            pl.when(c >= 2)(lambda: forward(c - 2))

            def tile_c(i, slot):
                part[slot_c, :, span(i * WIDE, WIDE)] = jnp.dot(act_buf[...], w_buf[slot, 0:ff, :], preferred_element_type=F32)

            tiles(n_c, base + n_a + n_b, 2, tile_c)
            start(moves(c)[0][:SUM_R])
            pl.when(c == 0)(lambda: gather_on(2))
            pl.when(c >= 1)(lambda: finish(c - 1))

        def at_trip(events):
            def service(i):
                for when, what in events:
                    pl.when(i == when)(lambda what=what: (what(), None)[1])

            return service

        def suffix_early():
            pass_on(P_OWN)
            pass_on(P_SIB)
            start(ring(EARLY)[:K_ON])

        @scoped("w_on")
        def w_on():
            for b, c in zip(w_brings, w_sends[ON_UP:]):
                b.wait_recv()
                c.start()
            start([w_share(UP), w_share(DOWN)])

        def suffix_late():
            pass_on(EARLY)
            start(ring(LATE)[:K_ON])

        @scoped("early_o")
        def early_o():
            swap(OE, True).wait_recv()
            start(gathers[0][0][:ON_UP] + o_keeps[:2])

        @scoped("w_rest")
        def w_rest():
            for i in (ON_UP, ON_DOWN):
                w_brings[i].wait_recv()
                w_share(i).start()

        def trip(step):
            return lax.div(step - lead, main_unroll)

        e_done = lax.div(b7 + main_unroll - 1, main_unroll)
        trips = (n_main - lead) // main_unroll
        events = [
            (trip(qt + 4), suffix_early),
            (trip(b2), lambda: [sides_here(P_OWN), sides_here(P_SIB)]),
            (trip(b4 - qt * pc), lambda: [far_here(P_OWN), far_here(P_SIB)]),
            (trip(b4 - 2 * qt), w_on),
            (trip(b4 - 4), suffix_late),
            (trip(b4), lambda: sides_here(EARLY)),
            (trip(jnp.where(chip < 2, b8, b6)), lambda: far_here(EARLY)),
            (e_done, lambda: finalize(0)),
            (e_done + 1, early_o),
            (trip(n_main - 32), lambda: [pass_on(LATE), w_last_round()]),
            (trip(b9), lambda: sides_here(LATE)),
            (trip(n_main - 20), w_rest),
        ]
        events.append((trip(n_main - 16), lambda: [gather_on(0), start(gathers[1][0][:ON_UP])]))
        far_late = trip(jnp.where(chip < 2, b9 + qt * (2 - chip), n_main))
        events.append((far_late, lambda: far_here(LATE)))
        if not exact:
            events.append((e_done + 2, sizes_meet))
        with jax.named_scope("run_main"):
            run(n_main, main_unroll, where, at_trip(events))

        pl.when(trip(b9) >= trips)(lambda: sides_here(LATE))
        pl.when(far_late >= trips)(lambda: far_here(LATE))
        with jax.named_scope("w_theirs"):
            for b in w_theirs:
                b.wait_recv()
        fetch(0)
        fetch(1)
        start_x(0)
        finalize(1)
        with jax.named_scope("o_on"):
            swap(OL, True).wait_recv()
            start(gathers[2][0][:ON_UP] + o_keeps[2:])
        loop(n_chunks, chunk_step)
        last = n_chunks - 1
        middle(last)
        forward(last - 1)
        finish(last)
        forward(last)
        if exact:
            plain_out[0, 0] = 1
        else:
            for c in size_on():
                c.wait_recv()
            top = jnp.max(jnp.max(size_tp[...], axis=0), axis=1)
            fits = (scale * scale * top[0] * top[1] <= S_LIMIT**2) & (top[2] <= 2.0**V_LIMIT)
            plain_out[0, 0] = fits.astype(jnp.int32)
        with jax.named_scope("tail"):
            for c in new_copies:
                c.wait()
            loop(n_chunks, drain)
            release(last - 1)
            release(last)
            for i in range(OL + 1):
                swap(i).wait_send()
            for item in (P_OWN, P_SIB, EARLY, LATE):
                for c in ring(item):
                    c.wait_send()
            for c in w_sends + [w_share(i) for i in range(4)] + [w_last(i) for i in range(3 * tps - 2)] + sum([g[0] for g in gathers], []):
                c.wait_send()
            if not exact:
                for c in size_copies() + size_on():
                    c.wait_send()

    n_state = 2 * side
    scratch = [
        pltpu.VMEM(shape, BF16)
        for shape in (
            (slots, d_in, WIDE), (2, TILE, d), (TILE, d), (TILE, d), (3, 2 * hd, side), (send_pre + pre, hd), (send_pre + pre, hd), (pre, 2, hd), (pre, 2, hd)
        )
    ]
    scratch += [pltpu.VMEM((SUB, n_state), F32), pltpu.VMEM((hd, n_state), F32)]
    scratch += [pltpu.VMEM(shape, BF16) for shape in ((2, blk, n_wide), (2, blk, ratio * hd))]
    scratch += [pltpu.VMEM((groups, SUB, LANES), F32), pltpu.VMEM((tps, SUB, LANES), F32)]
    scratch += [pltpu.VMEM((TILE, d_in), BF16), pltpu.VMEM((TILE, ff), BF16)]
    scratch += [pltpu.VMEM(shape, F32) for shape in ((2, TILE, d), (n_chunks, 2, half, d), (n_chunks, 2, quarter, d), (2, quarter, d))]
    scratch += [pltpu.VMEM((n_chunks, quarter, d), BF16)]
    if exact:
        scratch += [pltpu.VMEM((1, n_state), F32)]
    scratch += [dma(*n) for n in ((7,), (2,), (10,), (10,), (4, 6), (4, 6), (4,), (4,), (4,), (4,), (3, 4), (3, 4))]
    scratch += [dma(groups)] * 2 + [dma(tps)] * 2 + [dma(3 * tps - 2)] * 2 + [dma(slots, tps), dma(n_chunks, 10), dma(n_chunks, 10), dma(n_chunks)]
    shapes = [(rows, 2, hd)] * 2 + [(rows, d), (rows, d_in), (d_in, 2 * w_half), (tps - 1, w_rows, WIDE)]
    return pl.pallas_call(
        kernel,
        in_specs=[HBM] * 3 + [VMEM] * 3 + [HBM] * 4 + [VMEM] + [HBM] * 3,
        out_specs=[HBM] * 6 + [pl.BlockSpec(memory_space=pltpu.SMEM)],
        out_shape=[jax.ShapeDtypeStruct(s, BF16) for s in shapes] + [jax.ShapeDtypeStruct((1, 1), jnp.int32)],
        scratch_shapes=scratch,
        compiler_params=pltpu.CompilerParams(collective_id=2 + exact, has_side_effects=True, vmem_limit_bytes=VMEM_LIMIT),
        name="layer_exact" if exact else "layer",
    )(x_loc, kp2, vp2, cos_tab, sin_tab, norm_attn, w_query, w_key, w_value, w_out, norm_mlp, w_gate, w_up, w_down)


def angle_tables(owner, groups, blk, prefix_len, hd):
    lane = jnp.arange(hd, dtype=jnp.int32)
    early = lane < hd // 2
    block = jnp.where(early, owner, 2 * groups - 1 - owner)
    pos = prefix_len + block[None, :] * blk + jnp.arange(blk, dtype=jnp.int32)[:, None]
    inv_freq = ROPE_THETA ** (-jnp.arange(0, hd, 2, dtype=F32) / hd)
    angles = pos.astype(F32) * jnp.concatenate([inv_freq, inv_freq])[None, :]
    return jnp.cos(angles), jnp.sin(angles)


def solution(mesh):
    groups = mesh.shape["cp"]
    tps = mesh.shape["tp"]

    def local_layer(x_loc, kp_loc, vp_loc, norm_attn, w_query, w_key, w_value, w_out, norm_mlp, w_gate, w_up, w_down):
        rows = x_loc.shape[0]
        pre_dev, kv_loc, hd = kp_loc.shape
        tables = angle_tables(lax.axis_index("cp"), groups, rows // 2, pre_dev * groups, hd)

        def layer(exact):
            return layer_call(
                exact, x_loc, kp_loc, vp_loc, *tables, norm_attn, w_query, w_key, w_value, w_out, norm_mlp, w_gate, w_up, w_down, groups, tps
            )

        k_new, v_new, x_out, _, _, _, plain = layer(False)
        x_out = lax.cond(plain[0, 0] == 1, lambda: x_out, lambda: layer(True)[2])
        return x_out, k_new, v_new

    row_spec = P(("dp", "cp"), None)
    kv_spec = P(("dp", "cp"), "tp", None)
    col_spec = P(None, "tp")
    row_split = P("tp", None)
    vec_spec = P(None)
    return jax.shard_map(
        local_layer,
        mesh=mesh,
        in_specs=(row_spec, kv_spec, kv_spec, vec_spec, col_spec, col_spec, col_spec, row_split, vec_spec, col_spec, col_spec, row_split),
        out_specs=(row_spec, kv_spec, kv_spec),
        check_vma=False,
    )
```

time: 326 us -> 305 us (0.936)
  Pallas kernels: 312 us -> 294 us
  local copies, waits for them, and re-layouts: 11.1 us -> 7.61 us
    pallas_call x2 -> x1, Pallas kernels: 312 us -> 294 us  [layer_call(): pl.pallas_call(kernel, in_specs=[HBM] * 3 + [VMEM] * 3 + [HBM] * 4 + [VME...]
    reshape x3 -> x0, local copies, waits for them, and re-layouts: 5.2 us -> none  [the longest x1 2.33 us: attention(): vp_loc.reshape(flat)]
    unnamed x5 -> x7, local copies, waits for them, and re-layouts: 5.94 us -> 7.61 us
where the time goes in v2:
time: 305 us; the launch traced here: 304 us
  Pallas kernels  294 us (96%)
  local copies, waits for them, and re-layouts  7.61 us (2%)
    pallas_call x1, Pallas kernels, layer_call(): pl.pallas_call(kernel, in_specs=[HBM] * 3 + [VMEM] * 3 + [HBM] * 4 + [VME...  294 us
    unnamed x7, local copies, waits for them, and re-layouts  7.61 us

profile of v2, /device:TPU:97, one launch (start us, length us, event | category | flops | bytes accessed | tf_op | source)
XLA Modules:
  0.0 304.3 jit_solution(502386464395087626)
XLA Ops:
  0.7 0.1 pad_maximum_fusion
  0.7 1.7 fusion
  2.4 293.5 %layer.1 = (bf16[1024,2,128]{2,1,0:T(2,128)(2,1)}, bf16[1024,2,128]{2,1,0:T(2,128)(2,1)}, bf16[1024,3072]{1,0:T(8,128)(2,1)}, bf16[1024,3072]{1,0:T(8,128)(2,1)}...) custom-call(bf16[1024,3072]{1,0:T(8,128)(2,1)} %x_hbm.1, bf16[1024,2,128]{2,1,0:T(2,128)(2,1)} %kp_hbm.1, ...), custom_call_target="tpu_custom_call" | custom-call | tf_op jit(solution)/shard_map/layer/pallas_call | solution.py:887
  296.6 0.0 copy-start.1
  296.6 0.0 copy-start
  296.6 6.0 %copy.20 = bf16[1024,3072]{1,0:T(8,128)(2,1)} copy(bf16[1024,3072]{1,0:T(8,128)(2,1)} %get-tuple-element.66) | data formatting | bytes 12582912
  302.7 0.0 copy-done.1
  302.7 0.8 copy.21
  303.5 0.0 copy-done
  303.5 0.8 copy.22
  (3 shorter events, 0.0 us)
Async XLA Ops:
  296.6 6.0 %copy-start.1 = (bf16[1024,2,128]{2,1,0:T(2,128)(2,1)S(1)}, bf16[1024,2,128]{2,1,0:T(2,128)(2,1)}, u32[]{:S(2)}) copy-start(bf16[1024,2,128]{2,1,0:T(2,128)(2,1)} %get-tuple-element.64) | copy-start | bytes 1572868
  296.6 6.8 %copy-start = (bf16[1024,2,128]{2,1,0:T(2,128)(2,1)S(1)}, bf16[1024,2,128]{2,1,0:T(2,128)(2,1)}, u32[]{:S(2)}) copy-start(bf16[1024,2,128]{2,1,0:T(2,128)(2,1)} %get-tuple-element.65) | copy-start | bytes 1572868

commit v3 on v2

--- a/solution.py
+++ b/solution.py
@@ -12,6 +12,7 @@
 BF16 = jnp.bfloat16
 MESH = pl.DeviceIdType.MESH
 LANES = 128
+PAIR = 2
 SUB = 8
 TILE = 256
 NORM_ROWS = 32
@@ -75,7 +76,7 @@
 
 def gather_steps(at, sems, ranks, src=None):
     here, up, down, over, size = ranks
-    half = size // 2
+    half = size // PAIR
     to_up, to_down = {"tp": up}, {"tp": down}
 
     def move(i, rank, first, n, who, other=None):
@@ -99,23 +100,23 @@
 
 def layer_call(exact, x_loc, kp2, vp2, cos_tab, sin_tab, norm_attn, w_query, w_key, w_value, w_out, norm_mlp, w_gate, w_up, w_down, groups, tps):
     rows, d = x_loc.shape
-    blk = rows // 2
+    blk = rows // PAIR
     hd = kp2.shape[2]
     heads = w_query.shape[1] // hd
-    ratio = heads // 2
+    ratio = heads // PAIR
     pre = kp2.shape[0]
-    chips = groups // 2
+    chips = groups // PAIR
     assert chips == tps == 4 and pre == rows and hd == LANES and ratio == 3
-    deep = 2 * blk
+    deep = PAIR * blk
     n_wide = heads * hd
-    side = ratio * 2 * blk
-    half_side = side // 2
-    per_chip = 2 * pre
+    side = ratio * PAIR * blk
+    half_side = side // PAIR
+    per_chip = PAIR * pre
     suf = chips * per_chip
-    send = suf + chips * 2 * rows
+    send = suf + chips * PAIR * rows
     send_pre = send + rows
     d_out = w_out.shape[1]
-    w_half = (d_out - WIDE) // 2
+    w_half = (d_out - WIDE) // PAIR
     w_rows = w_out.shape[0]
     w_part = w_rows // groups
     scale = LOG2E * hd**-0.5
@@ -124,23 +125,23 @@
     ff = w_gate.shape[1]
     n_chunks = rows // TILE
     quarter = TILE // tps
-    half = quarter // 2
-    gate = WIDE // 2
+    half = quarter // PAIR
+    gate = WIDE // PAIR
     n_a, n_b, n_c = d // WIDE, ff // gate, d // WIDE
     per = n_a + n_b + n_c
     total = per * n_chunks
-    slots = 3
+    slots = 4
 
     def kernel(x_hbm, kp_hbm, vp_hbm, cos_ref, sin_ref, g_ref, wq_hbm, wk_hbm, wv_hbm, wo_hbm, g2_ref, wg_hbm, wu_hbm, wd_hbm,
                k_out, v_out, out_hbm, o_hbm, wall_hbm, wlast_hbm, plain_out,
                w_buf, x_buf, h_0, h_1, q3, keys, vals, kp_buf, vp_buf, l_ref, a_ref, o_st, o_snd, size_all, size_tp,
-               o_buf, act_buf, part, got1, got2, y_own, fin, *rest):
+               o_buf, act_buf, part, got1, got2, y_own, fin, flag, *rest):
         if exact:
             m_ref, *rest = rest
         l_sem, x_sem, sw_s, sw_r, x_s, x_r, w_s, w_r, d_s, d_r, o_s, o_r, z_s, z_r, y_s, y_r, e_s, e_r, t_sem, c_s, c_r, c_sem = rest
         me, t = lax.axis_index("cp"), lax.axis_index("tp")
         core, chip = both(me), lax.div(me, 2)
-        sib = {"cp": me + 1 - 2 * core}
+        sib = {"cp": me + 1 - PAIR * core}
         x_right, x_left = {"cp": lax.rem(me + 2, groups)}, {"cp": lax.rem(me + groups - 2, groups)}
         up, down, over = [lax.rem(t + j, tps) for j in (1, tps - 1, 2)]
 
@@ -152,7 +153,7 @@
 
         vp_copy = local(0, vp_hbm, vp_buf)
         kp_copy = local(1, kp_hbm, kp_buf)
-        pair_w = 2 * hd
+        pair_w = PAIR * hd
 
         def proj_w(pair):
             return pair * pair_w // WIDE, pl.ds(pair * pair_w % WIDE, pair_w)
@@ -179,21 +180,21 @@
         def part_rows(who):
             return span(who * w_part, w_part, SUB)
 
-        y_steps, x_steps, d_steps = range(tps - 1), range(tps - 1, 2 * (tps - 1)), range(2 * (tps - 1), 3 * tps - 2)
+        y_steps, x_steps, d_steps = range(tps - 1), range(tps - 1, PAIR * (tps - 1)), range(PAIR * (tps - 1), 3 * tps - 2)
 
         def w_last(i, arriving=False):
             if i in y_steps:
-                src = wo_hbm.at[part_rows(me), pl.ds(2 * w_half, WIDE)]
+                src = wo_hbm.at[part_rows(me), pl.ds(PAIR * w_half, WIDE)]
                 return remote(src, wlast_hbm.at[y_steps[-1] - i, part_rows(me)], (e_s, e_r), i, {"tp": lax.rem(t + i + 1, tps)})
-            back = 2 * (i - d_steps[0])
+            back = PAIR * (i - d_steps[0])
             if i in x_steps:
-                back = 2 * (i - y_steps[-1])
+                back = PAIR * (i - y_steps[-1])
                 to = {"cp": lax.rem(me + back, groups)}
                 owner = lax.rem(me + groups - back, groups) if arriving else me
             else:
                 to, owner = sib, lax.rem(me + groups - back, groups)
                 if arriving:
-                    owner = owner + 1 - 2 * core
+                    owner = owner + 1 - PAIR * core
             ref = wlast_hbm.at[:, part_rows(owner)]
             return remote(ref, ref, (e_s, e_r), i, to)
 
@@ -238,7 +239,7 @@
         def region(item, slot):
             if item in (P_OWN, P_SIB):
                 return pl.ds(slot * per_chip + item * pre, pre)
-            return pl.ds(suf + (2 * slot + item - EARLY) * deep, deep)
+            return pl.ds(suf + (PAIR * slot + item - EARLY) * deep, deep)
 
         def ring(item):
             plan = {K_RIGHT: (keys, 0, 1, x_right), V_RIGHT: (vals, 0, 1, x_right), K_LEFT: (keys, 0, 3, x_left), V_LEFT: (vals, 0, 3, x_left),
@@ -277,26 +278,26 @@
             late, sub = lax.div(i, blk // TILE), lax.rem(i, blk // TILE)
             at_rows = span(i * TILE, TILE)
             tab = span(sub * TILE, TILE)
-            first = lax.broadcasted_iota(jnp.int32, (TILE, hd), 1) < hd // 2
+            first = lax.broadcasted_iota(jnp.int32, (TILE, hd), 1) < hd // PAIR
 
             def table(ref):
                 v = ref[tab, :]
-                w = pltpu.roll(v, hd // 2, 1)
+                w = pltpu.roll(v, hd // PAIR, 1)
                 return jnp.where(first == (late == 0), v, w)
 
             cos, sin = table(cos_ref), table(sin_ref)
             sin = jnp.where(first, -sin, sin)
 
             def rope(v):
-                return v * cos + pltpu.roll(v, hd // 2, 1) * sin
+                return v * cos + pltpu.roll(v, hd // PAIR, 1) * sin
 
             for pair in range(n_proj // pair_w):
                 slot, w_lanes = proj_w(pair)
                 out = jnp.dot(h_tile[...], w_buf[slot, :, w_lanes], preferred_element_type=F32)
                 heads_new = []
-                for hh in range(2):
+                for hh in range(PAIR):
                     v = out[:, hh * hd : (hh + 1) * hd]
-                    head = 2 * pair + hh
+                    head = PAIR * pair + hh
                     at = jnp.where(core == hh, suf + late * deep, send + late * blk) + sub * TILE
                     if head < heads:
                         q_t = rope(v).astype(BF16).astype(F32).T
@@ -344,8 +345,8 @@
 
         def split_prefix(b):
             rows_b = span(b * LANES, LANES)
-            k, v = [buf[rows_b].reshape(LANES, 2 * hd) for buf in (kp_buf, vp_buf)]
-            for j in range(2):
+            k, v = [buf[rows_b].reshape(LANES, PAIR * hd) for buf in (kp_buf, vp_buf)]
+            for j in range(PAIR):
                 at = span(jnp.where(core == j, 0, send_pre) + b * LANES, LANES)
                 k_j, v_j = k[:, j * hd : (j + 1) * hd], v[:, j * hd : (j + 1) * hd].astype(F32)
                 keys[at, :] = k_j
@@ -354,10 +355,12 @@
                 note_size(2, v_j)
 
         loop(pre // LANES, split_prefix)
-        x_copy(0).wait()
+        with jax.named_scope("barrier"):
+            pl.semaphore_wait(barrier, len(greeted))
+        start([swap(KP), swap(VP)] + ring(P_OWN)[:K_ON] + [w_last(i) for i in y_steps] + w_sends[:ON_UP])
+        with jax.named_scope("x_wait"):
+            x_copy(0).wait()
         norm(0, 0)
-        pl.semaphore_wait(barrier, len(greeted))
-        start([swap(KP), swap(VP)] + ring(P_OWN)[:K_ON] + [w_last(i) for i in y_steps] + w_sends[:ON_UP])
         with jax.named_scope("w_wait"):
             for c in w_copies:
                 c.wait()
@@ -366,7 +369,7 @@
 
         @scoped("project")
         def two_tiles(j):
-            i = 2 * j
+            i = PAIR * j
             x_copy(i + 1).wait()
 
             @pl.when(i + 2 < n_tiles)
@@ -394,7 +397,7 @@
             def _():
                 start([swap(i) for i in (KE, VE, QE)])
 
-        loop(n_tiles // 2, two_tiles)
+        loop(n_tiles // PAIR, two_tiles)
         start([swap(i) for i in (KL, VL, QL)])
         new_copies = [local(4, kp_buf, k_out), local(5, vp_buf, v_out)]
         start(new_copies)
@@ -408,6 +411,16 @@
         def size_on():
             return [remote(size_tp.at[0], size_tp.at[j], (y_s, y_r), j, {"tp": lax.rem(t + j, tps)}) for j in range(1, tps)]
 
+        flag_copy = local(6, flag, plain_out)
+
+        def sizes_known():
+            for c in size_on():
+                c.wait_recv()
+            top = jnp.max(jnp.max(size_tp[...], axis=0), axis=1)
+            fits = (scale * scale * top[0] * top[1] <= S_LIMIT**2) & (top[2] <= 2.0**V_LIMIT)
+            flag[0, 0] = fits.astype(jnp.int32)
+            flag_copy.start()
+
         def sizes_meet():
             for c in size_copies():
                 c.wait_recv()
@@ -417,6 +430,8 @@
         if not exact:
             start(size_copies())
         if exact:
+            flag[0, 0] = 1
+            flag_copy.start()
             m_ref[...] = jnp.full_like(m_ref, -jnp.inf)
         l_ref[...] = jnp.zeros_like(l_ref)
         a_ref[...] = jnp.zeros_like(a_ref)
@@ -507,7 +522,7 @@
                 values(where(u), u % 2)
 
         def own_where(u):
-            who, rest = lax.div(u, 2 * ratio), lax.rem(u, 2 * ratio)
+            who, rest = lax.div(u, PAIR * ratio), lax.rem(u, PAIR * ratio)
             late, head = lax.div(rest, ratio), lax.rem(rest, ratio)
             return who, late, head, suf + late * deep
 
@@ -515,36 +530,36 @@
             who, late = step[:2]
             q_core = jnp.where(who == 0, core, 1 - core)
             seen = jnp.where(late == 0, q_core, 1 - q_core)
-            other = (2 * seen - 1) * blk
+            other = (PAIR * seen - 1) * blk
             return jnp.where(who == 0, 0, other), jnp.where(who == 0, other, 0)
 
         with jax.named_scope("run_own"):
             run(4 * ratio, 1 if exact else 2, own_where, lambda i: None, own_mask)
 
-        qt = 2 * ratio
+        qt = PAIR * ratio
         pc = per_chip // deep
         n_rem = chips - 1
         n_near = jnp.minimum(chip, 1) + lax.div(chip, n_rem)
-        b1 = 2 * qt * pc
+        b1 = PAIR * qt * pc
         b2 = b1 + qt
         b4 = b2 + n_rem * qt * pc
         b5 = b4 + qt * n_near
-        b6 = b5 + qt * pc
+        b6 = b5 + qt
         b7 = b6 + qt * (chip - n_near)
-        b8 = b7 + (n_rem - 1) * qt * pc
+        b8 = b7 + n_rem * qt * pc - qt
         b9 = b8 + qt * n_rem
-        n_main = b4 + n_rem * qt * pc + 2 * qt * n_rem
+        n_main = b4 + n_rem * qt * pc + PAIR * qt * n_rem
 
         def where(u):
-            def prefix(j, skip=0):
-                i, r = lax.div(j, qt * pc) + skip, lax.rem(j, qt * pc)
+            def prefix(j):
+                i, r = lax.div(j, qt * pc), lax.rem(j, qt * pc)
                 return lax.div(r, pc), far_last(i) * per_chip + lax.rem(r, pc) * deep
 
             def far_last(i):
                 return jnp.where(i == 0, 1, jnp.where(i == 1, n_rem, 2))
 
             def suffix(j, back):
-                return lax.rem(j, qt), suf + back * 2 * deep
+                return lax.rem(j, qt), suf + back * PAIR * deep
 
             tile = lax.div(u, pc)
             late = lax.div(tile, qt)
@@ -556,8 +571,8 @@
                 (b4, 0, suffix(u - b4, far_last(lax.div(u - b4, qt)))),
                 (b5, 1, prefix(u - b5)),
                 (b6, 0, suffix(u - b6, 2)),
-                (b7, 1, prefix(u - b7, 1)),
-                (b8, 1, (lax.div(u - b8, n_rem), suf + (1 + lax.rem(u - b8, n_rem)) * 2 * deep)),
+                (b7, 1, prefix(u - b7 + qt)),
+                (b8, 1, (lax.div(u - b8, n_rem), suf + (1 + lax.rem(u - b8, n_rem)) * PAIR * deep)),
                 (b9, 1, (j9[0], j9[1] + deep)),
             ):
                 here = u >= first
@@ -566,21 +581,15 @@
 
         @scoped("finalize")
         def finalize(h):
-            def one(u):
-                who, head = lax.div(u, ratio), lax.rem(u, ratio)
-                at = state_at((who, h, head))
-                inv = 1.0 / jnp.sum(l_ref[:, at], axis=0, keepdims=True)
-                o = (a_ref[:, at] * inv).T.astype(BF16)
-
-                @pl.when(who == 0)
-                def _():
-                    o_st[h, :, span(core * ratio * hd + head * hd, hd)] = o
-
-                @pl.when(who == 1)
-                def _():
-                    o_snd[h, :, span(head * hd, hd)] = o
-
-            loop(2 * ratio, one)
+            for who in range(PAIR):
+                for head in range(ratio):
+                    at = state_at((who, h, head))
+                    inv = 1.0 / jnp.sum(l_ref[:, at], axis=0, keepdims=True)
+                    o = (a_ref[:, at] * inv).T.astype(BF16)
+                    if who == 0:
+                        o_st[h, :, span(core * ratio * hd + head * hd, hd)] = o
+                    else:
+                        o_snd[h, :, span(head * hd, hd)] = o
             swap(OE + h).start()
 
         gathers, o_keeps = [], []
@@ -618,10 +627,15 @@
                 return [get(j, w.at[:, at], w_buf.at[slot, :, pl.ds(j * gate, gate)]) for j, w in enumerate((wg_hbm, wu_hbm))]
             return [get(0, wd_hbm.at[:, span(i * WIDE, WIDE)], w_buf.at[slot, pl.ds(0, ff)])]
 
+        def after_first():
+            swap(OL, True).wait_recv()
+            start(gathers[2][0][:ON_UP] + o_keeps[2:])
+            w_last_on()
+
         def fetch(g):
             i, slot = lax.rem(g, per), lax.rem(g, slots)
             last_a = n_a - 1
-            pl.when(g == 3)(w_last_on)
+            pl.when(g == slots)(after_first)
             pl.when(g == last_a)(w_last_here)
             for kind, first, n in ((0, 0, last_a), (3, last_a, 1), (1, n_a, n_b), (2, n_a + n_b, n_c)):
                 pl.when((g < total) & (i >= first) & (i < first + n))(lambda: start(tile_copies(kind, last_a if kind == 3 else i - first, slot)))
@@ -635,85 +649,97 @@
         def o_rows(c):
             return local(3, o_hbm.at[span(c * TILE, TILE)], o_buf)
 
-        def out_rows(c, q, first, n):
-            return out_hbm.at[span(c * TILE + q * quarter + first, n, half)]
-
-        def at_rows(q, first, n):
-            return span(q * quarter + first, n, half)
-
-        def moves(c):
+        def cols_of(cut):
+            return span(cut * d // PAIR, d // PAIR)
+
+        def moves(c, cut):
+            cols, slot = cols_of(cut), both(c)
+
             def go(i, src, dst):
-                return remote(src, dst, (c_s.at[c], c_r.at[c]), i, {"tp": up if i % 2 == 0 else down})
+                return remote(src, dst, (c_s.at[c, cut], c_r.at[c, cut]), i, {"tp": up if i % 2 == 0 else down})
 
             def mine(q, first):
-                return part.at[both(c), at_rows(q, first, half)]
-
-            top, low = pl.ds(0, half), pl.ds(half, half)
+                return part.at[slot, span(q * quarter + first, half, half), cols]
+
+            def out(q, first, n):
+                return out_hbm.at[span(c * TILE + q * quarter + first, n, half), cols]
+
+            def sums(way, first):
+                return got2.at[slot, way, pl.ds(first, half), cols]
+
+            done = fin.at[c, :, cols]
             sends = {
-                FAR_R: (mine(over, 0), got1.at[c, 0]),
-                FAR_L: (mine(over, half), got1.at[c, 1]),
-                NEAR_R: (mine(up, half), got2.at[c, 0, low]),
-                NEAR_L: (mine(down, 0), got2.at[c, 1, top]),
-                SUM_R: (mine(up, 0), got2.at[c, 0, top]),
-                SUM_L: (mine(down, half), got2.at[c, 1, low]),
-                OUT_R: (fin.at[c], out_rows(c, t, 0, quarter)),
-                OUT_L: (fin.at[c], out_rows(c, t, 0, quarter)),
-                ON_R: (out_rows(c, down, 0, half), out_rows(c, down, 0, half)),
-                ON_L: (out_rows(c, up, half, half), out_rows(c, up, half, half)),
+                FAR_R: (mine(over, 0), got1.at[slot, 0, :, cols]),
+                FAR_L: (mine(over, half), got1.at[slot, 1, :, cols]),
+                NEAR_R: (mine(up, half), sums(0, half)),
+                NEAR_L: (mine(down, 0), sums(1, 0)),
+                SUM_R: (mine(up, 0), sums(0, 0)),
+                SUM_L: (mine(down, half), sums(1, half)),
+                OUT_R: (done, out(t, 0, quarter)),
+                OUT_L: (done, out(t, 0, quarter)),
+                ON_R: (out(down, 0, half), out(down, 0, half)),
+                ON_L: (out(up, half, half), out(up, half, half)),
             }
             brings = {
-                OUT_R: (fin.at[c], out_rows(c, down, 0, quarter)),
-                OUT_L: (fin.at[c], out_rows(c, up, 0, quarter)),
-                ON_R: (out_rows(c, over, 0, half), out_rows(c, over, 0, half)),
-                ON_L: (out_rows(c, over, half, half), out_rows(c, over, half, half)),
+                OUT_R: (done, out(down, 0, quarter)),
+                OUT_L: (done, out(up, 0, quarter)),
+                ON_R: (out(over, 0, half), out(over, 0, half)),
+                ON_L: (out(over, half, half), out(over, half, half)),
             }
-            return [go(i, *s) for i, s in sends.items()], {i: go(i, *s) for i, s in brings.items()}
-
-        def own_copy(c):
-            return pltpu.make_async_copy(fin.at[c], out_rows(c, t, 0, quarter), c_sem.at[c])
-
-        @scoped("middle")
-        def middle(c):
-            m = moves(c)[0]
+            own = pltpu.make_async_copy(done, out(t, 0, quarter), c_sem.at[c, cut])
+            return [go(i, *m) for i, m in sends.items()], {i: go(i, *m) for i, m in brings.items()}, own
+
+        def cuts(name):
+            def deco(f):
+                return scoped(name)(lambda c: loop(2, lambda cut: f(c, cut)))
+
+            return deco
+
+        @cuts("middle")
+        def middle(c, cut):
+            m = moves(c, cut)[0]
             for way, q, first in ((0, up, 0), (1, down, half)):
                 m[FAR_R + way].wait_recv()
-                part[both(c), at_rows(q, first, half), :] += got1[c, way]
+                part[both(c), span(q * quarter + first, half, half), cols_of(cut)] += got1[both(c), way, :, cols_of(cut)]
                 m[SUM_R + way].start()
 
-        @scoped("finish")
-        def finish(c):
-            m = moves(c)[0]
+        @cuts("finish")
+        def finish(c, cut):
+            m, _, own = moves(c, cut)
             for i in (NEAR_R, NEAR_L, SUM_R, SUM_L):
                 m[i].wait_recv()
-            fin[c] = (y_own[both(c)] + (part[both(c), at_rows(t, 0, quarter), :] + (got2[c, 0] + got2[c, 1]))).astype(BF16)
-            own_copy(c).start()
+            cols, slot = cols_of(cut), both(c)
+            rest = got2[slot, 0, :, cols] + got2[slot, 1, :, cols]
+            fin[c, :, cols] = (y_own[slot, :, cols] + (part[slot, span(t * quarter, quarter, quarter), cols] + rest)).astype(BF16)
+            own.start()
             start(m[OUT_R:ON_R])
 
-        @scoped("forward")
-        def forward(c):
-            m, b = moves(c)
-            for way in range(2):
+        @cuts("forward")
+        def forward(c, cut):
+            m, b, _ = moves(c, cut)
+            for way in range(PAIR):
                 b[OUT_R + way].wait_recv()
                 m[ON_R + way].start()
 
-        @scoped("drain")
-        def drain(c):
-            m, b = moves(c)
+        @cuts("drain")
+        def drain(c, cut):
+            m, b, own = moves(c, cut)
             b[ON_R].wait_recv()
             b[ON_L].wait_recv()
             for s in m[OUT_R:]:
                 s.wait_send()
-            own_copy(c).wait()
-
-        def release(c):
-            for s in moves(c)[0][:OUT_R]:
+            own.wait()
+
+        @cuts("release")
+        def release(c, cut):
+            for s in moves(c, cut)[0][:OUT_R]:
                 s.wait_send()
 
         def tiles(n, base, kind, body):
             @scoped("tile_" + "abc"[kind])
             def one(i):
                 g = base + i
-                fetch(g + 2)
+                fetch(g + slots - 1)
                 slot = lax.rem(g, slots)
                 at = jnp.minimum(i, n_a - 2) if kind == 0 else i
                 for cp in tile_copies(kind, at, slot):
@@ -724,9 +750,9 @@
 
         def chunk_step(c):
             base, slot_c = c * per, both(c)
-            for i in range(3):
+            for i in (1, 2):
                 pl.when(c == i)(lambda i=i: gathered(i))
-            o_rows(c).start()
+            pl.when(c >= 1)(lambda: o_rows(c).start())
             pl.when(c >= 2)(lambda: release(c - 2))
             mlp_x(c).wait()
             pl.when(c + 1 < n_chunks)(lambda: start_x(c + 1))
@@ -756,10 +782,13 @@
 
             def tile_c(i, slot):
                 part[slot_c, :, span(i * WIDE, WIDE)] = jnp.dot(act_buf[...], w_buf[slot, 0:ff, :], preferred_element_type=F32)
+                for cut in range(PAIR):
+                    pl.when(i == (cut + 1) * n_c // PAIR - 1)(lambda cut=cut: start(moves(c, cut)[0][:SUM_R]))
 
             tiles(n_c, base + n_a + n_b, 2, tile_c)
-            start(moves(c)[0][:SUM_R])
             pl.when(c == 0)(lambda: gather_on(2))
+            if not exact:
+                pl.when(c == 1)(sizes_known)
             pl.when(c >= 1)(lambda: finish(c - 1))
 
         def at_trip(events):
@@ -796,6 +825,14 @@
                 w_brings[i].wait_recv()
                 w_share(i).start()
 
+        @scoped("first_tiles")
+        def first_tiles():
+            for b in w_theirs:
+                b.wait_recv()
+            start_x(0)
+            for g in range(slots - 1):
+                fetch(g)
+
         def trip(step):
             return lax.div(step - lead, main_unroll)
 
@@ -805,17 +842,18 @@
             (trip(qt + 4), suffix_early),
             (trip(b2), lambda: [sides_here(P_OWN), sides_here(P_SIB)]),
             (trip(b4 - qt * pc), lambda: [far_here(P_OWN), far_here(P_SIB)]),
-            (trip(b4 - 2 * qt), w_on),
+            (trip(b4 - qt), w_on),
             (trip(b4 - 4), suffix_late),
             (trip(b4), lambda: sides_here(EARLY)),
             (trip(jnp.where(chip < 2, b8, b6)), lambda: far_here(EARLY)),
             (e_done, lambda: finalize(0)),
             (e_done + 1, early_o),
-            (trip(n_main - 32), lambda: [pass_on(LATE), w_last_round()]),
+            (trip(n_main - 40), lambda: [pass_on(LATE), w_last_round()]),
             (trip(b9), lambda: sides_here(LATE)),
             (trip(n_main - 20), w_rest),
+            (trip(n_main - 8), first_tiles),
         ]
-        events.append((trip(n_main - 16), lambda: [gather_on(0), start(gathers[1][0][:ON_UP])]))
+        events.append((trip(n_main - 20), lambda: [gather_on(0), start(gathers[1][0][:ON_UP])]))
         far_late = trip(jnp.where(chip < 2, b9 + qt * (2 - chip), n_main))
         events.append((far_late, lambda: far_here(LATE)))
         if not exact:
@@ -825,32 +863,18 @@
 
         pl.when(trip(b9) >= trips)(lambda: sides_here(LATE))
         pl.when(far_late >= trips)(lambda: far_here(LATE))
-        with jax.named_scope("w_theirs"):
-            for b in w_theirs:
-                b.wait_recv()
-        fetch(0)
-        fetch(1)
-        start_x(0)
+        with jax.named_scope("gathered"):
+            gathered(0)
+        o_rows(0).start()
         finalize(1)
-        with jax.named_scope("o_on"):
-            swap(OL, True).wait_recv()
-            start(gathers[2][0][:ON_UP] + o_keeps[2:])
         loop(n_chunks, chunk_step)
         last = n_chunks - 1
         middle(last)
         forward(last - 1)
         finish(last)
         forward(last)
-        if exact:
-            plain_out[0, 0] = 1
-        else:
-            for c in size_on():
-                c.wait_recv()
-            top = jnp.max(jnp.max(size_tp[...], axis=0), axis=1)
-            fits = (scale * scale * top[0] * top[1] <= S_LIMIT**2) & (top[2] <= 2.0**V_LIMIT)
-            plain_out[0, 0] = fits.astype(jnp.int32)
         with jax.named_scope("tail"):
-            for c in new_copies:
+            for c in new_copies + [flag_copy]:
                 c.wait()
             loop(n_chunks, drain)
             release(last - 1)
@@ -866,28 +890,28 @@
                 for c in size_copies() + size_on():
                     c.wait_send()
 
-    n_state = 2 * side
+    n_state = PAIR * side
     scratch = [
         pltpu.VMEM(shape, BF16)
         for shape in (
-            (slots, d_in, WIDE), (2, TILE, d), (TILE, d), (TILE, d), (3, 2 * hd, side), (send_pre + pre, hd), (send_pre + pre, hd), (pre, 2, hd), (pre, 2, hd)
+            (slots, d_in, WIDE), (2, TILE, d), (TILE, d), (TILE, d), (3, PAIR * hd, side), (send_pre + pre, hd), (send_pre + pre, hd), (pre, 2, hd), (pre, 2, hd)
         )
     ]
     scratch += [pltpu.VMEM((SUB, n_state), F32), pltpu.VMEM((hd, n_state), F32)]
     scratch += [pltpu.VMEM(shape, BF16) for shape in ((2, blk, n_wide), (2, blk, ratio * hd))]
     scratch += [pltpu.VMEM((groups, SUB, LANES), F32), pltpu.VMEM((tps, SUB, LANES), F32)]
     scratch += [pltpu.VMEM((TILE, d_in), BF16), pltpu.VMEM((TILE, ff), BF16)]
-    scratch += [pltpu.VMEM(shape, F32) for shape in ((2, TILE, d), (n_chunks, 2, half, d), (n_chunks, 2, quarter, d), (2, quarter, d))]
-    scratch += [pltpu.VMEM((n_chunks, quarter, d), BF16)]
+    scratch += [pltpu.VMEM(shape, F32) for shape in ((2, TILE, d), (2, 2, half, d), (2, 2, quarter, d), (2, quarter, d))]
+    scratch += [pltpu.VMEM((n_chunks, quarter, d), BF16), pltpu.SMEM((1, 1), jnp.int32)]
     if exact:
         scratch += [pltpu.VMEM((1, n_state), F32)]
     scratch += [dma(*n) for n in ((7,), (2,), (10,), (10,), (4, 6), (4, 6), (4,), (4,), (4,), (4,), (3, 4), (3, 4))]
-    scratch += [dma(groups)] * 2 + [dma(tps)] * 2 + [dma(3 * tps - 2)] * 2 + [dma(slots, tps), dma(n_chunks, 10), dma(n_chunks, 10), dma(n_chunks)]
-    shapes = [(rows, 2, hd)] * 2 + [(rows, d), (rows, d_in), (d_in, 2 * w_half), (tps - 1, w_rows, WIDE)]
+    scratch += [dma(groups)] * 2 + [dma(tps)] * 2 + [dma(3 * tps - 2)] * 2 + [dma(slots, tps), dma(n_chunks, 2, 10), dma(n_chunks, 2, 10), dma(n_chunks, 2)]
+    shapes = [(rows, 2, hd)] * 2 + [(rows, d), (rows, d_in), (d_in, PAIR * w_half), (tps - 1, w_rows, WIDE)]
     return pl.pallas_call(
         kernel,
         in_specs=[HBM] * 3 + [VMEM] * 3 + [HBM] * 4 + [VMEM] + [HBM] * 3,
-        out_specs=[HBM] * 6 + [pl.BlockSpec(memory_space=pltpu.SMEM)],
+        out_specs=[HBM] * 7,
         out_shape=[jax.ShapeDtypeStruct(s, BF16) for s in shapes] + [jax.ShapeDtypeStruct((1, 1), jnp.int32)],
         scratch_shapes=scratch,
         compiler_params=pltpu.CompilerParams(collective_id=2 + exact, has_side_effects=True, vmem_limit_bytes=VMEM_LIMIT),
@@ -895,10 +919,36 @@
     )(x_loc, kp2, vp2, cos_tab, sin_tab, norm_attn, w_query, w_key, w_value, w_out, norm_mlp, w_gate, w_up, w_down)
 
 
+def emit_call(x_out, k_new, v_new):
+    step = x_out.shape[0] // SUB
+
+    def kernel(x_hbm, k_hbm, v_hbm, x_to, k_to, v_to, x_buf, k_buf, v_buf, r_sem, w_sem):
+        moves = [[ref.at[pl.ds(i * step, step)] for ref in (x_hbm, x_buf, x_to)] for i in range(SUB)]
+        moves += [(k_hbm, k_buf, k_to), (v_hbm, v_buf, v_to)]
+        reads = [pltpu.make_async_copy(src, buf, r_sem.at[i]) for i, (src, buf, _) in enumerate(moves)]
+        writes = [pltpu.make_async_copy(buf, dst, w_sem.at[i]) for i, (_, buf, dst) in enumerate(moves)]
+        start(reads)
+        for r, w in zip(reads, writes):
+            r.wait()
+            w.start()
+        for w in writes:
+            w.wait()
+
+    arrays = (x_out, k_new, v_new)
+    return pl.pallas_call(
+        kernel,
+        in_specs=[HBM] * len(arrays),
+        out_specs=[HBM] * len(arrays),
+        out_shape=[jax.ShapeDtypeStruct(a.shape, a.dtype) for a in arrays],
+        scratch_shapes=[pltpu.VMEM(a.shape, a.dtype) for a in arrays] + [dma(SUB + len(arrays))] * 2,
+        name="emit",
+    )(*arrays)
+
+
 def angle_tables(owner, groups, blk, prefix_len, hd):
     lane = jnp.arange(hd, dtype=jnp.int32)
-    early = lane < hd // 2
-    block = jnp.where(early, owner, 2 * groups - 1 - owner)
+    early = lane < hd // PAIR
+    block = jnp.where(early, owner, PAIR * groups - 1 - owner)
     pos = prefix_len + block[None, :] * blk + jnp.arange(blk, dtype=jnp.int32)[:, None]
     inv_freq = ROPE_THETA ** (-jnp.arange(0, hd, 2, dtype=F32) / hd)
     angles = pos.astype(F32) * jnp.concatenate([inv_freq, inv_freq])[None, :]
@@ -912,7 +962,7 @@
     def local_layer(x_loc, kp_loc, vp_loc, norm_attn, w_query, w_key, w_value, w_out, norm_mlp, w_gate, w_up, w_down):
         rows = x_loc.shape[0]
         pre_dev, kv_loc, hd = kp_loc.shape
-        tables = angle_tables(lax.axis_index("cp"), groups, rows // 2, pre_dev * groups, hd)
+        tables = angle_tables(lax.axis_index("cp"), groups, rows // PAIR, pre_dev * groups, hd)
 
         def layer(exact):
             return layer_call(
@@ -921,7 +971,7 @@
 
         k_new, v_new, x_out, _, _, _, plain = layer(False)
         x_out = lax.cond(plain[0, 0] == 1, lambda: x_out, lambda: layer(True)[2])
-        return x_out, k_new, v_new
+        return tuple(emit_call(x_out, k_new, v_new))
 
     row_spec = P(("dp", "cp"), None)
     kv_spec = P(("dp", "cp"), "tp", None)

time: 305 us -> 301 us (0.987)
  local copies, waits for them, and re-layouts: 7.61 us -> 0 us
    unnamed x7 -> x0, local copies, waits for them, and re-layouts: 7.61 us -> none
    pallas_call x0 -> x1, Pallas kernels: none -> 5.89 us  [emit_call(): pl.pallas_call(kernel, in_specs=[HBM] * len(arrays), out_specs=[HBM] * le...]
where the time goes in v3:
time: 301 us; the launch traced here: 300 us
  Pallas kernels  297 us (99%)
    pallas_call x1, Pallas kernels, layer_call(): pl.pallas_call(kernel, in_specs=[HBM] * 3 + [VMEM] * 3 + [HBM] * 4 + [VME...  291 us

profile of v3, /device:TPU:97, one launch (start us, length us, event | category | flops | bytes accessed | tf_op | source)
XLA Modules:
  0.0 300.5 jit_solution(8097051631057225536)
XLA Ops:
  0.7 0.1 pad_maximum_fusion
  0.7 1.7 fusion
  2.4 291.1 %layer.1 = (bf16[1024,2,128]{2,1,0:T(2,128)(2,1)}, bf16[1024,2,128]{2,1,0:T(2,128)(2,1)}, bf16[1024,3072]{1,0:T(8,128)(2,1)}, bf16[1024,3072]{1,0:T(8,128)(2,1)}...) custom-call(bf16[1024,3072]{1,0:T(8,128)(2,1)} %x_hbm.1, bf16[1024,2,128]{2,1,0:T(2,128)(2,1)} %kp_hbm.1, ...), custom_call_target="tpu_custom_call" | custom-call | tf_op jit(solution)/shard_map/layer/pallas_call | solution.py:911
  294.1 0.3 conditional.1
  294.4 5.9 %emit.1 = (bf16[1024,3072]{1,0:T(8,128)(2,1)}, bf16[1024,2,128]{2,1,0:T(2,128)(2,1)}, bf16[1024,2,128]{2,1,0:T(2,128)(2,1)}) custom-call(bf16[1024,3072]{1,0:T(8,128)(2,1)} %get-tuple-element.60.x_hbm, bf16[1024,2,128]{2,1,0:T(2,128)(2,1)} %get-tuple-element.56.k_hbm, bf16[1024,2,128]{2,1,0:T(2,128)(2,1)} %get-tuple-element.57.v_hbm), custom_call_target="tpu_custom_call" | custom-call | tf_op jit(solution)/shard_map/emit/pallas_call | solution.py:938
  (2 shorter events, 0.0 us)

commit v4 on v3

--- a/solution.py
+++ b/solution.py
@@ -1,5 +1,6 @@
 import jax
 import jax.numpy as jnp
+import numpy as np
 from jax import lax
 from jax.experimental import pallas as pl
 from jax.experimental.pallas import tpu as pltpu
@@ -98,7 +99,7 @@
     return sends, brings
 
 
-def layer_call(exact, x_loc, kp2, vp2, cos_tab, sin_tab, norm_attn, w_query, w_key, w_value, w_out, norm_mlp, w_gate, w_up, w_down, groups, tps):
+def layer_call(exact, x_loc, kp2, vp2, freq, norm_attn, w_query, w_key, w_value, w_out, norm_mlp, w_gate, w_up, w_down, groups, tps):
     rows, d = x_loc.shape
     blk = rows // PAIR
     hd = kp2.shape[2]
@@ -132,10 +133,10 @@
     total = per * n_chunks
     slots = 4
 
-    def kernel(x_hbm, kp_hbm, vp_hbm, cos_ref, sin_ref, g_ref, wq_hbm, wk_hbm, wv_hbm, wo_hbm, g2_ref, wg_hbm, wu_hbm, wd_hbm,
+    def kernel(x_hbm, kp_hbm, vp_hbm, freq_ref, g_ref, wq_hbm, wk_hbm, wv_hbm, wo_hbm, g2_ref, wg_hbm, wu_hbm, wd_hbm,
                k_out, v_out, out_hbm, o_hbm, wall_hbm, wlast_hbm, plain_out,
                w_buf, x_buf, h_0, h_1, q3, keys, vals, kp_buf, vp_buf, l_ref, a_ref, o_st, o_snd, size_all, size_tp,
-               o_buf, act_buf, part, got1, got2, y_own, fin, flag, *rest):
+               o_buf, act_buf, part, got1, got2, y_own, fin, flag, cos_ref, sin_ref, *rest):
         if exact:
             m_ref, *rest = rest
         l_sem, x_sem, sw_s, sw_r, x_s, x_r, w_s, w_r, d_s, d_r, o_s, o_r, z_s, z_r, y_s, y_r, e_s, e_r, t_sem, c_s, c_r, c_sem = rest
@@ -325,6 +326,17 @@
                 if heads_new:
                     (kp_buf, vp_buf)[pair - ratio][at_rows] = jnp.concatenate(heads_new, axis=1).reshape(TILE, 2, hd)
 
+        def angles(i):
+            shape, at = (NORM_ROWS, hd), span(i * NORM_ROWS, NORM_ROWS, NORM_ROWS)
+            early = lax.broadcasted_iota(jnp.int32, shape, 1) < hd // PAIR
+            row = lax.broadcasted_iota(jnp.int32, shape, 0) + i * NORM_ROWS
+            block = jnp.where(early, me, PAIR * groups - 1 - me)
+            angle = (pre * groups + block * blk + row).astype(F32) * freq_ref[...]
+            cos_ref[at, :] = jnp.cos(angle)
+            sin_ref[at, :] = jnp.sin(angle)
+
+        with jax.named_scope("angles"):
+            loop(blk // NORM_ROWS, angles)
         kp_copy.wait()
         vp_copy.wait()
         if not exact:
@@ -627,15 +639,10 @@
                 return [get(j, w.at[:, at], w_buf.at[slot, :, pl.ds(j * gate, gate)]) for j, w in enumerate((wg_hbm, wu_hbm))]
             return [get(0, wd_hbm.at[:, span(i * WIDE, WIDE)], w_buf.at[slot, pl.ds(0, ff)])]
 
-        def after_first():
-            swap(OL, True).wait_recv()
-            start(gathers[2][0][:ON_UP] + o_keeps[2:])
-            w_last_on()
-
         def fetch(g):
             i, slot = lax.rem(g, per), lax.rem(g, slots)
             last_a = n_a - 1
-            pl.when(g == slots)(after_first)
+            pl.when(g == slots)(w_last_on)
             pl.when(g == last_a)(w_last_here)
             for kind, first, n in ((0, 0, last_a), (3, last_a, 1), (1, n_a, n_b), (2, n_a + n_b, n_c)):
                 pl.when((g < total) & (i >= first) & (i < first + n))(lambda: start(tile_copies(kind, last_a if kind == 3 else i - first, slot)))
@@ -817,7 +824,7 @@
         @scoped("early_o")
         def early_o():
             swap(OE, True).wait_recv()
-            start(gathers[0][0][:ON_UP] + o_keeps[:2])
+            start(gathers[0][0][:ON_UP] + gathers[1][0][:ON_UP] + o_keeps[:2])
 
         @scoped("w_rest")
         def w_rest():
@@ -839,11 +846,11 @@
         e_done = lax.div(b7 + main_unroll - 1, main_unroll)
         trips = (n_main - lead) // main_unroll
         events = [
-            (trip(qt + 4), suffix_early),
+            (trip(qt), suffix_early),
             (trip(b2), lambda: [sides_here(P_OWN), sides_here(P_SIB)]),
             (trip(b4 - qt * pc), lambda: [far_here(P_OWN), far_here(P_SIB)]),
             (trip(b4 - qt), w_on),
-            (trip(b4 - 4), suffix_late),
+            (trip(b4 - qt), suffix_late),
             (trip(b4), lambda: sides_here(EARLY)),
             (trip(jnp.where(chip < 2, b8, b6)), lambda: far_here(EARLY)),
             (e_done, lambda: finalize(0)),
@@ -853,7 +860,7 @@
             (trip(n_main - 20), w_rest),
             (trip(n_main - 8), first_tiles),
         ]
-        events.append((trip(n_main - 20), lambda: [gather_on(0), start(gathers[1][0][:ON_UP])]))
+        events.append((trip(n_main - 8), lambda: gather_on(0)))
         far_late = trip(jnp.where(chip < 2, b9 + qt * (2 - chip), n_main))
         events.append((far_late, lambda: far_here(LATE)))
         if not exact:
@@ -863,10 +870,13 @@
 
         pl.when(trip(b9) >= trips)(lambda: sides_here(LATE))
         pl.when(far_late >= trips)(lambda: far_here(LATE))
+        finalize(1)
+        with jax.named_scope("late_o"):
+            swap(OL, True).wait_recv()
+            start(gathers[2][0][:ON_UP] + o_keeps[2:])
         with jax.named_scope("gathered"):
             gathered(0)
         o_rows(0).start()
-        finalize(1)
         loop(n_chunks, chunk_step)
         last = n_chunks - 1
         middle(last)
@@ -903,6 +913,7 @@
     scratch += [pltpu.VMEM((TILE, d_in), BF16), pltpu.VMEM((TILE, ff), BF16)]
     scratch += [pltpu.VMEM(shape, F32) for shape in ((2, TILE, d), (2, 2, half, d), (2, 2, quarter, d), (2, quarter, d))]
     scratch += [pltpu.VMEM((n_chunks, quarter, d), BF16), pltpu.SMEM((1, 1), jnp.int32)]
+    scratch += [pltpu.VMEM((blk, hd), F32)] * PAIR
     if exact:
         scratch += [pltpu.VMEM((1, n_state), F32)]
     scratch += [dma(*n) for n in ((7,), (2,), (10,), (10,), (4, 6), (4, 6), (4,), (4,), (4,), (4,), (3, 4), (3, 4))]
@@ -910,13 +921,13 @@
     shapes = [(rows, 2, hd)] * 2 + [(rows, d), (rows, d_in), (d_in, PAIR * w_half), (tps - 1, w_rows, WIDE)]
     return pl.pallas_call(
         kernel,
-        in_specs=[HBM] * 3 + [VMEM] * 3 + [HBM] * 4 + [VMEM] + [HBM] * 3,
+        in_specs=[HBM] * 3 + [VMEM] * 2 + [HBM] * 4 + [VMEM] + [HBM] * 3,
         out_specs=[HBM] * 7,
         out_shape=[jax.ShapeDtypeStruct(s, BF16) for s in shapes] + [jax.ShapeDtypeStruct((1, 1), jnp.int32)],
         scratch_shapes=scratch,
         compiler_params=pltpu.CompilerParams(collective_id=2 + exact, has_side_effects=True, vmem_limit_bytes=VMEM_LIMIT),
         name="layer_exact" if exact else "layer",
-    )(x_loc, kp2, vp2, cos_tab, sin_tab, norm_attn, w_query, w_key, w_value, w_out, norm_mlp, w_gate, w_up, w_down)
+    )(x_loc, kp2, vp2, freq, norm_attn, w_query, w_key, w_value, w_out, norm_mlp, w_gate, w_up, w_down)
 
 
 def emit_call(x_out, k_new, v_new):
@@ -945,16 +956,6 @@
     )(*arrays)
 
 
-def angle_tables(owner, groups, blk, prefix_len, hd):
-    lane = jnp.arange(hd, dtype=jnp.int32)
-    early = lane < hd // PAIR
-    block = jnp.where(early, owner, PAIR * groups - 1 - owner)
-    pos = prefix_len + block[None, :] * blk + jnp.arange(blk, dtype=jnp.int32)[:, None]
-    inv_freq = ROPE_THETA ** (-jnp.arange(0, hd, 2, dtype=F32) / hd)
-    angles = pos.astype(F32) * jnp.concatenate([inv_freq, inv_freq])[None, :]
-    return jnp.cos(angles), jnp.sin(angles)
-
-
 def solution(mesh):
     groups = mesh.shape["cp"]
     tps = mesh.shape["tp"]
@@ -962,11 +963,11 @@
     def local_layer(x_loc, kp_loc, vp_loc, norm_attn, w_query, w_key, w_value, w_out, norm_mlp, w_gate, w_up, w_down):
         rows = x_loc.shape[0]
         pre_dev, kv_loc, hd = kp_loc.shape
-        tables = angle_tables(lax.axis_index("cp"), groups, rows // PAIR, pre_dev * groups, hd)
+        freq = jnp.asarray(np.tile(ROPE_THETA ** (-np.arange(0, hd, PAIR) / hd), PAIR)[None, :], F32)
 
         def layer(exact):
             return layer_call(
-                exact, x_loc, kp_loc, vp_loc, *tables, norm_attn, w_query, w_key, w_value, w_out, norm_mlp, w_gate, w_up, w_down, groups, tps
+                exact, x_loc, kp_loc, vp_loc, freq, norm_attn, w_query, w_key, w_value, w_out, norm_mlp, w_gate, w_up, w_down, groups, tps
             )
 
         k_new, v_new, x_out, _, _, _, plain = layer(False)

time: 301 us -> 298 us (0.990)
  no operation moved by 1% of the time
where the time goes in v4:
time: 298 us
  Pallas kernels  296 us (99%)
    pallas_call x1, Pallas kernels, layer_call(): pl.pallas_call(kernel, in_specs=[HBM] * 3 + [VMEM] * 2 + [HBM] * 4 + [VME...  290 us

profile of v4, /device:TPU:97, one launch (start us, length us, event | category | flops | bytes accessed | tf_op | source)
XLA Modules:
  0.0 298.1 jit_solution(4453804102074423627)
XLA Ops:
  0.6 290.4 %layer.1 = (bf16[1024,2,128]{2,1,0:T(2,128)(2,1)}, bf16[1024,2,128]{2,1,0:T(2,128)(2,1)}, bf16[1024,3072]{1,0:T(8,128)(2,1)}, bf16[1024,3072]{1,0:T(8,128)(2,1)}...) custom-call(bf16[1024,3072]{1,0:T(8,128)(2,1)} %x_hbm.1, bf16[1024,2,128]{2,1,0:T(2,128)(2,1)} %kp_hbm.1, ...), custom_call_target="tpu_custom_call" | custom-call | tf_op jit(solution)/shard_map/layer/pallas_call | solution.py:922
  291.7 0.3 conditional.1
  292.0 5.9 %emit.1 = (bf16[1024,3072]{1,0:T(8,128)(2,1)}, bf16[1024,2,128]{2,1,0:T(2,128)(2,1)}, bf16[1024,2,128]{2,1,0:T(2,128)(2,1)}) custom-call(bf16[1024,3072]{1,0:T(8,128)(2,1)} %get-tuple-element.55.x_hbm, bf16[1024,2,128]{2,1,0:T(2,128)(2,1)} %get-tuple-element.53.k_hbm, bf16[1024,2,128]{2,1,0:T(2,128)(2,1)} %get-tuple-element.54.v_hbm), custom_call_target="tpu_custom_call" | custom-call | tf_op jit(solution)/shard_map/emit/pallas_call | solution.py:949

commit v5 on v4

--- a/solution.py
+++ b/solution.py
@@ -824,7 +824,7 @@
         @scoped("early_o")
         def early_o():
             swap(OE, True).wait_recv()
-            start(gathers[0][0][:ON_UP] + gathers[1][0][:ON_UP] + o_keeps[:2])
+            start(gathers[0][0][:ON_UP] + o_keeps[:2])
 
         @scoped("w_rest")
         def w_rest():
@@ -860,7 +860,7 @@
             (trip(n_main - 20), w_rest),
             (trip(n_main - 8), first_tiles),
         ]
-        events.append((trip(n_main - 8), lambda: gather_on(0)))
+        events.append((trip(n_main - 12), lambda: [gather_on(0), start(gathers[1][0][:ON_UP])]))
         far_late = trip(jnp.where(chip < 2, b9 + qt * (2 - chip), n_main))
         events.append((far_late, lambda: far_here(LATE)))
         if not exact:

time: 298 us -> 303 us (1.017)
  Pallas kernels: 296 us -> 301 us
    pallas_call x1, Pallas kernels: 290 us -> 295 us  [layer_call(): pl.pallas_call(kernel, in_specs=[HBM] * 3 + [VMEM] * 2 + [HBM] * 4 + [VME...]
where the time goes in v5:
time: 303 us; the launch traced here: 302 us
  Pallas kernels  301 us (99%)
    pallas_call x1, Pallas kernels, layer_call(): pl.pallas_call(kernel, in_specs=[HBM] * 3 + [VMEM] * 2 + [HBM] * 4 + [VME...  295 us

profile of v5, /device:TPU:97, one launch (start us, length us, event | category | flops | bytes accessed | tf_op | source)
XLA Modules:
  0.0 302.4 jit_solution(5373884844101589422)
XLA Ops:
  0.6 294.7 %layer.1 = (bf16[1024,2,128]{2,1,0:T(2,128)(2,1)}, bf16[1024,2,128]{2,1,0:T(2,128)(2,1)}, bf16[1024,3072]{1,0:T(8,128)(2,1)}, bf16[1024,3072]{1,0:T(8,128)(2,1)}...) custom-call(bf16[1024,3072]{1,0:T(8,128)(2,1)} %x_hbm.1, bf16[1024,2,128]{2,1,0:T(2,128)(2,1)} %kp_hbm.1, ...), custom_call_target="tpu_custom_call" | custom-call | tf_op jit(solution)/shard_map/layer/pallas_call | solution.py:922
  296.0 0.3 conditional.1
  296.3 5.9 %emit.1 = (bf16[1024,3072]{1,0:T(8,128)(2,1)}, bf16[1024,2,128]{2,1,0:T(2,128)(2,1)}, bf16[1024,2,128]{2,1,0:T(2,128)(2,1)}) custom-call(bf16[1024,3072]{1,0:T(8,128)(2,1)} %get-tuple-element.55.x_hbm, bf16[1024,2,128]{2,1,0:T(2,128)(2,1)} %get-tuple-element.53.k_hbm, bf16[1024,2,128]{2,1,0:T(2,128)(2,1)} %get-tuple-element.54.v_hbm), custom_call_target="tpu_custom_call" | custom-call | tf_op jit(solution)/shard_map/emit/pallas_call | solution.py:949
